TPU v7x, 32 devices: a whole 2x2x4 slice. The times are simulated.
32 devices in a mesh: gx: 8 (over z, x), gy: 4 (over y, core).
Axes of the slice: x: 2, y: 2, z: 4, core: 2. Of those that a mesh axis runs over, the one named last changes fastest.
Arguments:
- right_side: float32 [3, 224, 12432], P(None, 'gx', 'gy'), may hold values from -6 to 6
- guess: float32 [3, 224, 12432], P(None, 'gx', 'gy'), may hold values from -6 to 6
- material: int32 [32, 16, 16], P('gx', 'gy'), may hold values from 0 to 7
- lame: float32 [2, 8], replicated, may hold values from 0.5 to 2
- upper: float32 [1], replicated, may hold values from 3 to 6
- lower_ratio: float32 [1], replicated, may hold values from 0.05 to 0.3
Outputs:
- smoothed: float32 [3, 224, 12432], P(None, 'gx', 'gy')
- residual: float32 [3, 224, 12432], P(None, 'gx', 'gy')
All inputs are finite; a program needn't handle non-finite values.
Results may differ from a plain program's by a relative error of at most 0.0003.
Values sent between devices are 32-bit elements; how exact they have to be, the bound alone decides.
A program may use at most 128 MiB of HBM per device.

v0:
```python
import jax
import jax.numpy as jnp
import numpy as np
from jax import lax
from jax.experimental import pallas as pl
from jax.experimental.pallas import tpu as pltpu
from jax.sharding import PartitionSpec as P

DEG = 7
SWEEPS = 2
CHEB = 3


highest = lax.Precision.HIGHEST


def legendre_pair(points, degree):
    prev_poly = points * 0.0 + 1.0
    this_poly = points * 1.0
    for order in range(2, degree + 1):
        next_poly = ((2 * order - 1) * points * this_poly - (order - 1) * prev_poly) / order
        prev_poly = this_poly
        this_poly = next_poly
    return (this_poly, prev_poly)


def gll_tables(degree):
    count = degree + 1
    points = -np.cos(np.pi * np.arange(count) / degree)
    for newton_step in range(60):
        this_poly, prev_poly = legendre_pair(points, degree)
        points = points - (points * this_poly - prev_poly) / (count * this_poly)
    values, unused_poly = legendre_pair(points, degree)
    weights = 2.0 / (degree * (degree + 1) * values**2)
    identity_np = np.eye(count)
    spacing = points[:, None] - points[None, :] + identity_np
    derivative = values[:, None] / (values[None, :] * spacing) * (1.0 - identity_np)
    derivative[0, 0] = -degree * (degree + 1) / 4.0
    derivative[degree, degree] = degree * (degree + 1) / 4.0
    stiff_ratio = (weights[:, None] * derivative**2).sum(0) / weights
    return (weights, derivative, stiff_ratio)


def clamped_gather(blocks):
    free_nodes = DEG * blocks - 1
    selector = np.zeros((free_nodes, blocks * (DEG + 1)), np.float32)
    for element in range(blocks):
        for node_idx in range(DEG + 1):
            target = DEG * element + node_idx - 1
            if 0 <= target < free_nodes:
                selector[target, element * (DEG + 1) + node_idx] = 1.0
    return selector


N1 = DEG + 1
SLOTS = 4


def halves(value):
    high = value.astype(jnp.bfloat16)
    low = (value - high.astype(jnp.float32)).astype(jnp.bfloat16)
    return high, low


def np_halves(matrix):
    high = np.asarray(matrix, np.float32).astype(jnp.bfloat16)
    low = (np.asarray(matrix, np.float64) - high.astype(np.float64)).astype(jnp.bfloat16)
    return high, low


def apply_pairs(matrix, values):
    half = N1 // 2
    even = [values[i] + values[DEG - i] for i in range(half)]
    odd = [values[i] - values[DEG - i] for i in range(half)]
    outs = [None] * N1
    for p in range(half):
        plus = None
        minus = None
        for i in range(half):
            by_even = float(np.float32((matrix[p, i] + matrix[p, DEG - i]) / 2))
            by_odd = float(np.float32((matrix[p, i] - matrix[p, DEG - i]) / 2))
            plus = by_even * even[i] if plus is None else plus + by_even * even[i]
            minus = by_odd * odd[i] if minus is None else minus + by_odd * odd[i]
        outs[p] = minus + plus
        outs[DEG - p] = minus - plus
    return outs


def smoother_kernel(
    steps,
    elems_x,
    elems_y,
    derivative,
    lame,
    upper,
    lower_ratio,
    guess_in,
    source_in,
    material,
    weight_in,
    own_in,
    sum_in,
    spread_in,
    gather_in,
    select_in,
    grad_in,
    back_in,
    join_in,
    smoothed_out,
    residual_out,
    coef,
    field,
    resid,
    source,
    lam_w,
    mu_w,
    inverse,
    change,
    grad_x,
    grad_y,
    grad_z,
    flat_a,
    flat_b,
    send_x,
    send_y,
    send_c,
    recv_x,
    recv_y,
    recv_c,
    send_sem,
    recv_sem,
):
    cols = elems_x * elems_y
    size_x = lax.axis_size("gx")
    size_y = lax.axis_size("gy")
    me_x = lax.axis_index("gx")
    me_y = lax.axis_index("gy")
    near_x = (lax.rem(me_x + size_x - 1, size_x), lax.rem(me_x + 1, size_x))
    near_y = (lax.rem(me_y + size_y - 1, size_y), lax.rem(me_y + 1, size_y))
    partners = [(near_x[0], me_y), (near_x[1], me_y), (me_x, near_y[0]), (me_x, near_y[1])]
    partners += [(near_x[a], near_y[b]) for a in range(2) for b in range(2)]

    barrier = pltpu.get_barrier_semaphore()
    for partner in partners:
        pl.semaphore_signal(
            barrier, inc=1, device_id=partner, device_id_type=pl.DeviceIdType.MESH
        )
    pl.semaphore_wait(barrier, len(partners))

    def copies(slot, c):
        made = []
        for d in range(8):
            if d < 2:
                src, dst = send_x.at[slot, c, d], recv_x.at[slot, c, 1 - d]
            elif d < 4:
                src, dst = send_y.at[slot, c, d - 2], recv_y.at[slot, c, 3 - d]
            else:
                src, dst = send_c.at[slot, c, d - 4], recv_c.at[slot, c, 7 - d]
            mirror = (1, 0, 3, 2, 7, 6, 5, 4)[d]
            made.append(
                pltpu.make_async_remote_copy(
                    src_ref=src,
                    dst_ref=dst,
                    send_sem=send_sem.at[slot, c, d],
                    recv_sem=recv_sem.at[slot, c, mirror],
                    device_id=partners[d],
                    device_id_type=pl.DeviceIdType.MESH,
                )
            )
        return made

    rows = lax.broadcasted_iota(jnp.int32, (N1 * cols, 128), 0) % cols
    row_x = rows % elems_x
    inner_low_y = rows >= elems_x
    inner_high_y = rows < cols - elems_x
    inner_low_x = row_x >= 1
    inner_high_x = row_x < elems_x - 1
    last_x = elems_x - 1
    last_y = cols - elems_x
    flat = (N1 * cols, 128)
    full = (N1, cols, 128)

    def local_sum(ref, c):
        zero = jnp.zeros(flat, jnp.float32)
        low = ref[c, 0].reshape(flat)
        high = ref[c, DEG].reshape(flat)
        to_low = jnp.where(inner_low_x, pltpu.roll(high, 1, 0), zero)
        to_high = jnp.where(inner_high_x, pltpu.roll(low, N1 * cols - 1, 0), zero)
        ref[c, 0] = (low + to_low).reshape(full)
        ref[c, DEG] = (high + to_high).reshape(full)
        low = ref[c, :, 0].reshape(flat)
        high = ref[c, :, DEG].reshape(flat)
        to_low = jnp.where(inner_low_y, pltpu.roll(high, elems_x, 0), zero)
        to_high = jnp.where(inner_high_y, pltpu.roll(low, N1 * cols - elems_x, 0), zero)
        ref[c, :, 0] = (low + to_low).reshape(full)
        ref[c, :, DEG] = (high + to_high).reshape(full)

    def post(ref, slot, c):
        send_y[slot, c, 0] = ref[c, :, 0, 0:elems_x, :]
        send_y[slot, c, 1] = ref[c, :, DEG, last_y:cols, :]
        for b in range(elems_y):
            at = b * elems_x
            send_x[slot, c, 0, :, b : b + 1, :] = ref[c, 0, :, at : at + 1, :]
            at = b * elems_x + last_x
            send_x[slot, c, 1, :, b : b + 1, :] = ref[c, DEG, :, at : at + 1, :]
        for a in range(2):
            for b in range(2):
                at = a * last_x + b * last_y
                send_c[slot, c, 2 * a + b] = ref[c, a * DEG, b * DEG, at : at + 1, :]
        for copy in copies(slot, c):
            copy.start()

    def collect(ref, slot, c):
        for copy in copies(slot, c):
            copy.wait()
        ref[c, :, 0, 0:elems_x, :] += recv_y[slot, c, 0]
        ref[c, :, DEG, last_y:cols, :] += recv_y[slot, c, 1]
        for b in range(elems_y):
            at = b * elems_x
            ref[c, 0, :, at : at + 1, :] += recv_x[slot, c, 0, :, b : b + 1, :]
            at = b * elems_x + last_x
            ref[c, DEG, :, at : at + 1, :] += recv_x[slot, c, 1, :, b : b + 1, :]
        for a in range(2):
            for b in range(2):
                at = a * last_x + b * last_y
                ref[c, a * DEG, b * DEG, at : at + 1, :] += recv_c[slot, c, 2 * a + b]

    nodes_x = DEG * elems_x
    nodes_y = DEG * elems_y
    nodes_z = guess_in.shape[2] // nodes_y
    pad_x = flat_a.shape[1]
    zeros_big = jnp.zeros((N1, cols, 128), jnp.float32)

    @pl.loop(0, nodes_y)
    def _(y):
        flat_a[y] = jnp.zeros((pad_x, 128), jnp.float32)
        flat_b[y] = jnp.zeros((pad_x, 128), jnp.float32)

    def through(src, dst, matrix):
        @pl.loop(0, elems_y, unroll=elems_y)
        def _(b):
            pick = pl.ds(b * DEG, DEG)
            parts = halves(src[pick].reshape(DEG * pad_x, 128))
            dst[pick] = jnp.dot(
                jnp.concatenate(parts, axis=1), matrix[...], preferred_element_type=jnp.float32
            ).reshape(DEG, pad_x, 128)

    def enter(flat_in, ref, c):
        lines = flat_in[c]
        for y in range(nodes_y):
            flat_a[y, 0:nodes_x, 0:nodes_z] = lines[:, y * nodes_z : (y + 1) * nodes_z]
        through(flat_a, flat_b, gather_in)
        ref[c, DEG] = zeros_big
        ref[c, :, DEG] = zeros_big
        for b in range(elems_y):
            for j in range(DEG):
                for i in range(DEG):
                    ref[c, i, j, b * elems_x : (b + 1) * elems_x, :] = flat_b[
                        b * DEG + j, pl.ds(i, elems_x, stride=DEG), :
                    ]

    def leave(ref, flat_out, c):
        for b in range(elems_y):
            for j in range(DEG):
                for i in range(DEG):
                    flat_b[b * DEG + j, pl.ds(i, elems_x, stride=DEG), :] = ref[
                        c, i, j, b * elems_x : (b + 1) * elems_x, :
                    ]
        through(flat_b, flat_a, select_in)
        lines = [flat_a[y, 0:nodes_x, 0:nodes_z] for y in range(nodes_y)]
        flat_out[c] = jnp.concatenate(lines, axis=1)

    @pl.loop(0, 3)
    def _(c):
        enter(guess_in, field, c)
        local_sum(field, c)
        post(field, 0, c)

    upper_edge = jnp.full((1, 128), upper[0], jnp.float32)
    lower_edge = lower_ratio[0] * upper_edge
    center = (upper_edge + lower_edge) / 2.0
    radius = (upper_edge - lower_edge) / 2.0
    sigma_ratio = center / radius
    for sweep in range(SWEEPS):
        coef[0, sweep * CHEB] = jnp.zeros((1, 128), jnp.float32)
        coef[1, sweep * CHEB] = 1.0 / center
        factor = 1.0 / sigma_ratio
        for later in range(1, CHEB):
            factor_next = 1.0 / (2.0 * sigma_ratio - factor)
            coef[0, sweep * CHEB + later] = factor_next * factor
            coef[1, sweep * CHEB + later] = 2.0 * factor_next / radius
            factor = factor_next

    kinds = jnp.concatenate([material[:, b, :] for b in range(elems_y)], axis=0)
    tables = []
    for row in range(2):
        picked = jnp.zeros(kinds.shape, jnp.float32)
        for kind in range(lame.shape[1]):
            picked = jnp.where(kinds == kind, lame[row, kind], picked)
        tables.append(
            jnp.dot(picked, spread_in[...], precision=highest, preferred_element_type=jnp.float32)
        )
    lam_all, mu_all = tables

    @pl.loop(0, N1)
    def _(i):
        for j in range(N1):
            lam_w[i, j] = lam_all * weight_in[i, j]
            mu_w[i, j] = mu_all * weight_in[i, j]

    @pl.loop(0, 3 * N1, unroll=N1)
    def _(at):
        c = at // N1
        i = at % N1
        pieces = []
        for j in range(N1):
            own = own_in[c, i, j]
            pieces.append(lam_w[i, j] * own + mu_w[i, j] * (sum_in[i, j] + own))
        high, low = halves(jnp.concatenate(pieces, axis=0))
        summed = jnp.dot(
            jnp.concatenate([high, low], axis=1), join_in[...], preferred_element_type=jnp.float32
        )
        inverse[c, i] = summed.reshape(N1, cols, 128)

    for c in range(3):
        local_sum(inverse, c)
        post(inverse, 1, c)

    def gradients(c):
        @pl.loop(0, N1, unroll=N1)
        def _(i):
            high, low = halves(field[c, i].reshape(flat))
            both = jnp.dot(
                jnp.concatenate([high, low], axis=1),
                grad_in[...],
                preferred_element_type=jnp.float32,
            )
            for p, out in enumerate(apply_pairs(derivative, [field[c, k, i] for k in range(N1)])):
                grad_x[c, p, i] = out
            for q, out in enumerate(apply_pairs(derivative, [field[c, i, k] for k in range(N1)])):
                grad_y[c, i, q] = out
            grad_z[c, i] = (both[:, :128] + both[:, 128:]).reshape(full)

    def stresses():
        @pl.loop(0, N1, unroll=N1)
        def _(i):
            for j in range(N1):
                lam = lam_w[i, j]
                mu = mu_w[i, j]
                d00, d11, d22 = grad_x[0, i, j], grad_y[1, i, j], grad_z[2, i, j]
                base = lam * (d00 + d11 + d22)
                two = mu + mu
                grad_x[0, i, j] = two * d00 + base
                grad_y[1, i, j] = two * d11 + base
                grad_z[2, i, j] = two * d22 + base
                s01 = mu * (grad_x[1, i, j] + grad_y[0, i, j])
                s02 = mu * (grad_x[2, i, j] + grad_z[0, i, j])
                s12 = mu * (grad_y[2, i, j] + grad_z[1, i, j])
                grad_x[1, i, j] = s01
                grad_y[0, i, j] = s01
                grad_x[2, i, j] = s02
                grad_z[0, i, j] = s02
                grad_y[2, i, j] = s12
                grad_z[1, i, j] = s12

    def forces(c):
        @pl.loop(0, N1, unroll=N1)
        def _(j):
            for p, out in enumerate(apply_pairs(derivative.T, [grad_x[c, k, j] for k in range(N1)])):
                resid[c, p, j] = out

        @pl.loop(0, N1, unroll=N1)
        def _(i):
            outs = apply_pairs(derivative.T, [grad_y[c, i, k] for k in range(N1)])
            inner = jnp.concatenate([resid[c, i, q] + outs[q] for q in range(N1)], axis=0)
            parts = halves(grad_z[c, i].reshape(flat)) + halves(inner)
            both = jnp.dot(
                jnp.concatenate(parts, axis=1), back_in[...], preferred_element_type=jnp.float32
            )
            resid[c, i] = source[c, i] - (both[:, :128] + both[:, 128:]).reshape(full)

    def residuals(slot):
        stresses()

        @pl.loop(0, 3)
        def _(c):
            forces(c)
            local_sum(resid, c)
            post(resid, slot, c)

    @pl.loop(0, 3)
    def _(c):
        enter(source_in, source, c)

    @pl.loop(0, 3)
    def _(c):
        collect(field, 0, c)
        gradients(c)

    @pl.loop(0, 3)
    def _(c):
        collect(inverse, 1, c)

        @pl.loop(0, N1)
        def _(i):
            inverse[c, i] = 1.0 / inverse[c, i]
            change[c, i] = zeros_big

    @pl.loop(0, steps)
    def _(step):
        slot = 2 + step % 2
        residuals(slot)

        @pl.loop(0, 3)
        def _(c):
            collect(resid, slot, c)
            alpha = coef[0, step]
            beta = coef[1, step]

            @pl.loop(0, N1, unroll=N1)
            def _(i):
                new = alpha * change[c, i] + beta * (inverse[c, i] * resid[c, i])
                change[c, i] = new
                field[c, i] += new

            gradients(c)

    slot = 2 + steps % 2
    residuals(slot)

    @pl.loop(0, 3)
    def _(c):
        leave(field, smoothed_out, c)

    @pl.loop(0, 3)
    def _(c):
        collect(resid, slot, c)
        leave(resid, residual_out, c)


def z_join(blocks, clamped):
    nodes = DEG * blocks + 1
    gather = np.zeros((nodes, blocks * N1))
    for element in range(blocks):
        for k in range(N1):
            gather[DEG * element + k, element * N1 + k] = 1.0
    if clamped:
        gather[0] = 0.0
        gather[nodes - 1] = 0.0
    return gather.T @ gather


def local(right_side, guess, material, lame, upper, lower_ratio):
    elems_x, elems_y, elems_z = material.shape
    cols = elems_x * elems_y
    lanes = N1 * elems_z
    nodes_z = DEG * elems_z - 1
    weights_np, derivative_np, ratio_np = gll_tables(DEG)
    eye_z = np.eye(elems_z)
    grad_np = np.kron(eye_z, derivative_np.T)
    join_np = z_join(elems_z, True)
    back_np = np.kron(eye_z, derivative_np) @ join_np
    grad_high, grad_low = np_halves(grad_np)
    back_high, back_low = np_halves(back_np)
    none = np.zeros_like(grad_high)
    joined = join_np.astype(jnp.bfloat16)
    grad_in = jnp.asarray(np.block([[grad_high, grad_low], [grad_high, none]]))
    back_in = jnp.asarray(
        np.block([[back_high, back_low], [back_high, none], [joined, none], [joined, none]])
    )
    all_join = z_join(elems_z, False).astype(jnp.bfloat16)
    join_in = jnp.asarray(np.concatenate([all_join, all_join], axis=0))

    weights_z = np.tile(weights_np, elems_z)
    ratio_z = np.tile(ratio_np, elems_z)
    weight_np = weights_np[:, None, None] * weights_np[None, :, None] * weights_z
    shape_w = (N1, N1, lanes)
    own_x = np.broadcast_to(ratio_np[:, None, None], shape_w)
    own_y = np.broadcast_to(ratio_np[None, :, None], shape_w)
    own_z = np.broadcast_to(ratio_z, shape_w)
    own_np = np.stack([own_x, own_y, own_z])
    weight_in = jnp.asarray(weight_np[:, :, None], jnp.float32)
    own_in = jnp.asarray(own_np[:, :, :, None], jnp.float32)
    sum_in = jnp.asarray((own_x + own_y + own_z)[:, :, None], jnp.float32)

    gather_np = clamped_gather(elems_z)
    nodes_z = gather_np.shape[0]
    owned_np = gather_np.copy()
    owned_np[:, DEG::N1] = 0.0
    enter_np = np.zeros((lanes, lanes))
    enter_np[:nodes_z] = gather_np
    leave_np = np.zeros((lanes, lanes))
    leave_np[:, :nodes_z] = owned_np.T
    gather_in = jnp.asarray(np.concatenate([enter_np, enter_np], axis=0).astype(jnp.bfloat16))
    select_in = jnp.asarray(np.concatenate([leave_np, leave_np], axis=0).astype(jnp.bfloat16))
    spread_in = jnp.asarray(np.kron(eye_z, np.ones((1, N1))), dtype=jnp.float32)

    pad_x = -(-DEG * elems_x // 8) * 8
    whole = (3, N1, N1, cols, lanes)
    vmem = pl.BlockSpec(memory_space=pltpu.VMEM)
    smem = pl.BlockSpec(memory_space=pltpu.SMEM)
    big = pltpu.VMEM(whole, jnp.float32)
    small = pltpu.VMEM((N1, N1, cols, lanes), jnp.float32)
    lines = pltpu.VMEM((DEG * elems_y, pad_x, lanes), jnp.float32)
    face_x = pltpu.VMEM((SLOTS, 3, 2, N1, elems_y, lanes), jnp.float32)
    face_y = pltpu.VMEM((SLOTS, 3, 2, N1, elems_x, lanes), jnp.float32)
    corner = pltpu.VMEM((SLOTS, 3, 4, 1, lanes), jnp.float32)
    shape = jax.ShapeDtypeStruct(guess.shape, jnp.float32)

    def kernel(*refs):
        smoother_kernel(SWEEPS * CHEB, elems_x, elems_y, derivative_np, *refs)

    return pl.pallas_call(
        kernel,
        out_shape=(shape, shape),
        in_specs=[smem] * 3 + [vmem] * 12,
        out_specs=(vmem, vmem),
        scratch_shapes=[pltpu.VMEM((2, SWEEPS * CHEB, 1, lanes), jnp.float32)]
        + [big] * 3
        + [small] * 2
        + [big] * 5
        + [lines] * 2
        + [face_x, face_y, corner] * 2
        + [pltpu.SemaphoreType.DMA((SLOTS, 3, 8))] * 2,
        compiler_params=pltpu.CompilerParams(collective_id=0, has_side_effects=True),
    )(
        lame,
        upper,
        lower_ratio,
        guess,
        right_side,
        material,
        weight_in,
        own_in,
        sum_in,
        spread_in,
        gather_in,
        select_in,
        grad_in,
        back_in,
        join_in,
    )


def solution(mesh):
    placed = (P(None, "gx", "gy"), P(None, "gx", "gy"), P("gx", "gy", None), P(), P(), P())
    return jax.shard_map(
        local,
        mesh=mesh,
        in_specs=placed,
        out_specs=(P(None, "gx", "gy"), P(None, "gx", "gy")),
        check_vma=False,
    )
```

profile of v0, /device:TPU:0, one launch (start us, length us, event | category | flops | bytes accessed | tf_op | source)
XLA Modules:
  0.0 78.0 jit_solution(13085812233169320994)
XLA Ops:
  1.9 72.5 %shard_map.158 = (f32[3,28,3108]{2,1,0:T(8,128)}, f32[3,28,3108]{2,1,0:T(8,128)}) custom-call(f32[2,8]{1,0:T(2,128)} %refs_0_.1, f32[1]{0:T(128)S(6)} %copy.19.refs_1_, f32[1]{0:T(128)S(6)} %copy.20.refs_2_, f32[3,28,3108]{2,1,0:T(8,128)} %refs_3_.1, f32[3,28,3108]{2,1,0:T(8,128)} %refs_4_.1, s32[4,4,16]{2,1,0:T(4,128)} %refs_5_.1, ...), custom_call_target="tpu_custom_call" | custom-call | tf_op jit(solution)/shard_map/pallas_call | solution.py:513
  74.4 0.0 copy-start
  74.4 2.5 %copy.21 = f32[3,28,3108]{2,1,0:T(8,128)} copy(f32[3,28,3108]{2,1,0:T(8,128)} %get-tuple-element.4) | data formatting | bytes 2088576
  76.9 0.0 copy-done
  76.9 1.0 %copy.22 = f32[3,28,3108]{2,1,0:T(8,128)} copy(f32[3,28,3108]{2,1,0:T(8,128)S(1)} %copy-done) | data formatting | bytes 2088576
Async XLA Ops:
  74.4 2.5 %copy-start = (f32[3,28,3108]{2,1,0:T(8,128)S(1)}, f32[3,28,3108]{2,1,0:T(8,128)}, u32[]{:S(2)}) copy-start(f32[3,28,3108]{2,1,0:T(8,128)} %get-tuple-element.5) | copy-start | bytes 3132868
where the time goes:
time: 78.1 us; the launch traced here: 78 us
  Pallas kernels  72.5 us (93%)
  local copies, waits for them, and re-layouts  3.53 us (5%)
  between operations  1.94 us (2%)
    pallas_call x1, Pallas kernels, local(): pl.pallas_call(kernel, out_shape=(shape, shape), in_specs=[smem] * 3 + [v...  72.5 us
    unnamed x4, local copies, waits for them, and re-layouts  3.53 us

commit v1 on v0

--- a/solution.py
+++ b/solution.py
@@ -54,6 +54,7 @@
 
 N1 = DEG + 1
 SLOTS = 4
+UNROLL = 6
 
 
 def halves(value):
@@ -68,7 +69,7 @@
     return high, low
 
 
-def apply_pairs(matrix, values):
+def apply_pairs(matrix, values, parity):
     half = N1 // 2
     even = [values[i] + values[DEG - i] for i in range(half)]
     odd = [values[i] - values[DEG - i] for i in range(half)]
@@ -82,15 +83,21 @@
             plus = by_even * even[i] if plus is None else plus + by_even * even[i]
             minus = by_odd * odd[i] if minus is None else minus + by_odd * odd[i]
         outs[p] = minus + plus
-        outs[DEG - p] = minus - plus
+        outs[DEG - p] = plus - minus if parity > 0 else minus - plus
     return outs
+
+
+def element_tables():
+    weights, derivative, ratio = gll_tables(DEG)
+    own = derivative.T * weights[None, :] / weights[:, None]
+    second = own @ derivative
+    return weights, derivative, ratio, own, second
 
 
 def smoother_kernel(
     steps,
     elems_x,
     elems_y,
-    derivative,
     lame,
     upper,
     lower_ratio,
@@ -103,8 +110,10 @@
     spread_in,
     gather_in,
     select_in,
-    grad_in,
-    back_in,
+    edge_in,
+    own_mat,
+    back_mat,
+    second_mat,
     join_in,
     smoothed_out,
     residual_out,
@@ -116,9 +125,10 @@
     mu_w,
     inverse,
     change,
-    grad_x,
-    grad_y,
-    grad_z,
+    along_x,
+    own_z,
+    stress_x,
+    part_x,
     flat_a,
     flat_b,
     send_x,
@@ -145,7 +155,6 @@
         pl.semaphore_signal(
             barrier, inc=1, device_id=partner, device_id_type=pl.DeviceIdType.MESH
         )
-    pl.semaphore_wait(barrier, len(partners))
 
     def copies(slot, c):
         made = []
@@ -274,6 +283,11 @@
     def _(c):
         enter(guess_in, field, c)
         local_sum(field, c)
+
+    pl.semaphore_wait(barrier, len(partners))
+
+    @pl.loop(0, 3)
+    def _(c):
         post(field, 0, c)
 
     upper_edge = jnp.full((1, 128), upper[0], jnp.float32)
@@ -326,76 +340,147 @@
         local_sum(inverse, c)
         post(inverse, 1, c)
 
-    def gradients(c):
-        @pl.loop(0, N1, unroll=N1)
-        def _(i):
-            high, low = halves(field[c, i].reshape(flat))
-            both = jnp.dot(
-                jnp.concatenate([high, low], axis=1),
-                grad_in[...],
-                preferred_element_type=jnp.float32,
-            )
-            for p, out in enumerate(apply_pairs(derivative, [field[c, k, i] for k in range(N1)])):
-                grad_x[c, p, i] = out
-            for q, out in enumerate(apply_pairs(derivative, [field[c, i, k] for k in range(N1)])):
-                grad_y[c, i, q] = out
-            grad_z[c, i] = (both[:, :128] + both[:, 128:]).reshape(full)
-
-    def stresses():
-        @pl.loop(0, N1, unroll=N1)
-        def _(i):
-            for j in range(N1):
-                lam = lam_w[i, j]
-                mu = mu_w[i, j]
-                d00, d11, d22 = grad_x[0, i, j], grad_y[1, i, j], grad_z[2, i, j]
-                base = lam * (d00 + d11 + d22)
-                two = mu + mu
-                grad_x[0, i, j] = two * d00 + base
-                grad_y[1, i, j] = two * d11 + base
-                grad_z[2, i, j] = two * d22 + base
-                s01 = mu * (grad_x[1, i, j] + grad_y[0, i, j])
-                s02 = mu * (grad_x[2, i, j] + grad_z[0, i, j])
-                s12 = mu * (grad_y[2, i, j] + grad_z[1, i, j])
-                grad_x[1, i, j] = s01
-                grad_y[0, i, j] = s01
-                grad_x[2, i, j] = s02
-                grad_z[0, i, j] = s02
-                grad_y[2, i, j] = s12
-                grad_z[1, i, j] = s12
-
-    def forces(c):
+    weights, derivative, _, own, second = element_tables()
+    edge = float(np.float32(1.0 / weights[0]))
+    groups = [slice(8 * h, 8 * h + 8) for h in range(cols // 8)]
+
+    def product(parts, matrix):
+        both = jnp.dot(
+            jnp.concatenate(parts, axis=1), matrix[...], preferred_element_type=jnp.float32
+        )
+        return (both[:, :128] + both[:, 128:]).reshape(full)
+
+    def forward(c, j, values):
+        if c == 2:
+            own_z[:, j] = product(halves(values.reshape(flat)), own_mat)
+        for rows in groups:
+            lines = [values[i, rows] for i in range(N1)]
+            outs = apply_pairs(own, lines, -1) if c == 0 else apply_pairs(second, lines, 1)
+            for i in range(N1):
+                along_x[c, i, j, rows] = outs[i]
+
+    def begin(c):
         @pl.loop(0, N1, unroll=N1)
         def _(j):
-            for p, out in enumerate(apply_pairs(derivative.T, [grad_x[c, k, j] for k in range(N1)])):
-                resid[c, p, j] = out
+            forward(c, j, field[c, :, j])
+
+    def advance(c, step):
+        alpha = coef[0, step]
+        beta = coef[1, step]
 
         @pl.loop(0, N1, unroll=N1)
+        def _(j):
+            new = alpha * change[c, :, j] + beta * (inverse[c, :, j] * resid[c, :, j])
+            change[c, :, j] = new
+            new = field[c, :, j] + new
+            field[c, :, j] = new
+            forward(c, j, new)
+
+    def sheet(i, edge_x):
+        lines_y = []
+        lines_v = []
+        lines_z = []
+        lines_t = []
+        edge_z = edge_in[...]
+        for rows in groups:
+            u_x = [field[0, i, j, rows] for j in range(N1)]
+            u_y = [field[1, i, j, rows] for j in range(N1)]
+            u_z = [field[2, i, j, rows] for j in range(N1)]
+            g_y = apply_pairs(own, u_y, -1)
+            second_x = apply_pairs(second, u_x, 1)
+            second_z = apply_pairs(second, u_z, 1)
+            extra_y = []
+            t_y = []
+            group_v = []
+            group_z = []
+            group_t = []
+            for j in range(N1):
+                lam = lam_w[i, j, rows]
+                mu = mu_w[i, j, rows]
+                g_x = along_x[0, i, j, rows]
+                g_z = own_z[i, j, rows]
+                g_xy = g_x + g_y[j]
+                total = g_xy + g_z
+                e_z = edge_z * u_z[j]
+                div = e_z - total
+                own_x = -g_x
+                own_y = -g_y[j]
+                left = second_x[j]
+                right = along_x[1, i, j, rows]
+                if edge_x is not None:
+                    e_x = edge_x * u_x[j]
+                    div = div + e_x
+                    own_x = (e_x + e_x) - g_x
+                    left = left + edge_x * (g_y[j] + g_z)
+                if j in (0, DEG):
+                    edge_y = -edge if j == 0 else edge
+                    e_y = edge_y * u_y[j]
+                    div = div + e_y
+                    own_y = (e_y + e_y) - g_y[j]
+                    right = right + edge_y * (g_x + g_z)
+                base = lam * div - mu * total
+                stress_x[i, j, rows] = base + mu * own_x
+                part_x[i, j, rows] = mu * left
+                t_y.append(base + mu * own_y)
+                extra_y.append(mu * right)
+                group_v.append(mu * u_y[j])
+                group_t.append(base + mu * ((e_z + e_z) - g_z))
+                group_z.append(mu * ((along_x[2, i, j, rows] + second_z[j]) + edge_z * g_xy))
+            back_y = apply_pairs(derivative.T, t_y, -1)
+            lines_y.append([back_y[j] + extra_y[j] for j in range(N1)])
+            lines_v.append(group_v)
+            lines_z.append(group_z)
+            lines_t.append(group_t)
+
+        def stacked(lines):
+            return jnp.concatenate([lines[h][j] for j in range(N1) for h in range(len(groups))], axis=0)
+
+        parts = halves(stacked(lines_y)) + halves(stacked(lines_v))
+        resid[1, i] = source[1, i] - product(parts, second_mat)
+        parts = halves(stacked(lines_z)) + halves(stacked(lines_t))
+        resid[2, i] = source[2, i] - product(parts, back_mat)
+
+    def closing(j):
+        lines_x = []
+        lines_v = []
+        for rows in groups:
+            back_x = apply_pairs(derivative.T, [stress_x[i, j, rows] for i in range(N1)], -1)
+            lines_x.append([part_x[i, j, rows] + back_x[i] for i in range(N1)])
+            lines_v.append([mu_w[i, j, rows] * field[0, i, j, rows] for i in range(N1)])
+
+        def stacked(lines):
+            return jnp.concatenate([lines[h][i] for i in range(N1) for h in range(len(groups))], axis=0)
+
+        parts = halves(stacked(lines_x)) + halves(stacked(lines_v))
+        resid[0, :, j] = source[0, :, j] - product(parts, second_mat)
+
+    def residuals(slot):
+        @pl.loop(1, DEG, unroll=UNROLL)
         def _(i):
-            outs = apply_pairs(derivative.T, [grad_y[c, i, k] for k in range(N1)])
-            inner = jnp.concatenate([resid[c, i, q] + outs[q] for q in range(N1)], axis=0)
-            parts = halves(grad_z[c, i].reshape(flat)) + halves(inner)
-            both = jnp.dot(
-                jnp.concatenate(parts, axis=1), back_in[...], preferred_element_type=jnp.float32
-            )
-            resid[c, i] = source[c, i] - (both[:, :128] + both[:, 128:]).reshape(full)
-
-    def residuals(slot):
-        stresses()
-
-        @pl.loop(0, 3)
+            sheet(i, None)
+
+        for side in range(2):
+            sheet(side * DEG, edge if side else -edge)
+
+        @pl.loop(1, 3)
         def _(c):
-            forces(c)
             local_sum(resid, c)
             post(resid, slot, c)
+
+        @pl.loop(0, N1, unroll=N1)
+        def _(j):
+            closing(j)
+
+        local_sum(resid, 0)
+        post(resid, slot, 0)
 
     @pl.loop(0, 3)
     def _(c):
         enter(source_in, source, c)
 
-    @pl.loop(0, 3)
-    def _(c):
+    for c in (1, 2, 0):
         collect(field, 0, c)
-        gradients(c)
+        begin(c)
 
     @pl.loop(0, 3)
     def _(c):
@@ -411,19 +496,9 @@
         slot = 2 + step % 2
         residuals(slot)
 
-        @pl.loop(0, 3)
-        def _(c):
+        for c in (1, 2, 0):
             collect(resid, slot, c)
-            alpha = coef[0, step]
-            beta = coef[1, step]
-
-            @pl.loop(0, N1, unroll=N1)
-            def _(i):
-                new = alpha * change[c, i] + beta * (inverse[c, i] * resid[c, i])
-                change[c, i] = new
-                field[c, i] += new
-
-            gradients(c)
+            advance(c, step)
 
     slot = 2 + steps % 2
     residuals(slot)
@@ -455,19 +530,26 @@
     cols = elems_x * elems_y
     lanes = N1 * elems_z
     nodes_z = DEG * elems_z - 1
-    weights_np, derivative_np, ratio_np = gll_tables(DEG)
+    weights_np, derivative_np, ratio_np, own_np_1, second_np = element_tables()
     eye_z = np.eye(elems_z)
-    grad_np = np.kron(eye_z, derivative_np.T)
     join_np = z_join(elems_z, True)
+    joined = join_np.astype(jnp.bfloat16)
+
+    def exact_pair(matrix):
+        high, low = np_halves(matrix)
+        none = np.zeros_like(high)
+        return [[high, low], [high, none]]
+
+    exact_join = [[joined, np.zeros_like(joined)]] * 2
+    own_mat = jnp.asarray(np.block(exact_pair(np.kron(eye_z, own_np_1.T))))
     back_np = np.kron(eye_z, derivative_np) @ join_np
-    grad_high, grad_low = np_halves(grad_np)
-    back_high, back_low = np_halves(back_np)
-    none = np.zeros_like(grad_high)
-    joined = join_np.astype(jnp.bfloat16)
-    grad_in = jnp.asarray(np.block([[grad_high, grad_low], [grad_high, none]]))
-    back_in = jnp.asarray(
-        np.block([[back_high, back_low], [back_high, none], [joined, none], [joined, none]])
-    )
+    back_mat = jnp.asarray(np.block(exact_join + exact_pair(back_np)))
+    scaled_np = np.kron(eye_z, second_np) @ join_np
+    second_mat = jnp.asarray(np.block(exact_join + exact_pair(scaled_np)))
+    edge_np = np.zeros((1, lanes))
+    edge_np[0, 0::N1] = -1.0 / weights_np[0]
+    edge_np[0, DEG::N1] = 1.0 / weights_np[DEG]
+    edge_in = jnp.asarray(edge_np, jnp.float32)
     all_join = z_join(elems_z, False).astype(jnp.bfloat16)
     join_in = jnp.asarray(np.concatenate([all_join, all_join], axis=0))
 
@@ -508,17 +590,18 @@
     shape = jax.ShapeDtypeStruct(guess.shape, jnp.float32)
 
     def kernel(*refs):
-        smoother_kernel(SWEEPS * CHEB, elems_x, elems_y, derivative_np, *refs)
+        smoother_kernel(SWEEPS * CHEB, elems_x, elems_y, *refs)
 
     return pl.pallas_call(
         kernel,
         out_shape=(shape, shape),
-        in_specs=[smem] * 3 + [vmem] * 12,
+        in_specs=[smem] * 3 + [vmem] * 14,
         out_specs=(vmem, vmem),
         scratch_shapes=[pltpu.VMEM((2, SWEEPS * CHEB, 1, lanes), jnp.float32)]
         + [big] * 3
         + [small] * 2
-        + [big] * 5
+        + [big] * 3
+        + [small] * 3
         + [lines] * 2
         + [face_x, face_y, corner] * 2
         + [pltpu.SemaphoreType.DMA((SLOTS, 3, 8))] * 2,
@@ -536,8 +619,10 @@
         spread_in,
         gather_in,
         select_in,
-        grad_in,
-        back_in,
+        edge_in,
+        own_mat,
+        back_mat,
+        second_mat,
         join_in,
     )
 

time: 78.1 us -> 75.6 us (0.968)
  Pallas kernels: 72.5 us -> 69.9 us
    pallas_call x1, Pallas kernels: 72.5 us -> 69.9 us  [local(): pl.pallas_call(kernel, out_shape=(shape, shape), in_specs=[smem] * 3 + [v...]
where the time goes in v1:
time: 75.6 us; the launch traced here: 75.4 us
  Pallas kernels  69.9 us (92%)
  local copies, waits for them, and re-layouts  3.53 us (5%)
  between operations  1.94 us (3%)
    pallas_call x1, Pallas kernels, local(): pl.pallas_call(kernel, out_shape=(shape, shape), in_specs=[smem] * 3 + [v...  69.9 us
    unnamed x4, local copies, waits for them, and re-layouts  3.53 us

profile of v1, /device:TPU:0, one launch (start us, length us, event | category | flops | bytes accessed | tf_op | source)
XLA Modules:
  0.0 75.4 jit_solution(1189485374471200532)
XLA Ops:
  1.9 69.9 %shard_map.176 = (f32[3,28,3108]{2,1,0:T(8,128)}, f32[3,28,3108]{2,1,0:T(8,128)}) custom-call(f32[2,8]{1,0:T(2,128)} %refs_0_.1, f32[1]{0:T(128)S(6)} %copy.21.refs_1_, f32[1]{0:T(128)S(6)} %copy.22.refs_2_, f32[3,28,3108]{2,1,0:T(8,128)} %refs_3_.1, f32[3,28,3108]{2,1,0:T(8,128)} %refs_4_.1, s32[4,4,16]{2,1,0:T(4,128)} %refs_5_.1, ...), custom_call_target="tpu_custom_call" | custom-call | tf_op jit(solution)/shard_map/pallas_call | solution.py:595
  71.9 0.0 copy-start
  71.9 2.5 %copy.23 = f32[3,28,3108]{2,1,0:T(8,128)} copy(f32[3,28,3108]{2,1,0:T(8,128)} %get-tuple-element.4) | data formatting | bytes 2088576
  74.4 0.0 copy-done
  74.4 1.0 %copy.24 = f32[3,28,3108]{2,1,0:T(8,128)} copy(f32[3,28,3108]{2,1,0:T(8,128)S(1)} %copy-done) | data formatting | bytes 2088576
Async XLA Ops:
  71.9 2.5 %copy-start = (f32[3,28,3108]{2,1,0:T(8,128)S(1)}, f32[3,28,3108]{2,1,0:T(8,128)}, u32[]{:S(2)}) copy-start(f32[3,28,3108]{2,1,0:T(8,128)} %get-tuple-element.5) | copy-start | bytes 3132868

commit v2 on v1

--- a/solution.py
+++ b/solution.py
@@ -53,7 +53,7 @@
 
 
 N1 = DEG + 1
-SLOTS = 4
+SLOTS = 3
 UNROLL = 6
 
 
@@ -114,6 +114,7 @@
     own_mat,
     back_mat,
     second_mat,
+    exact_mat,
     join_in,
     smoothed_out,
     residual_out,
@@ -129,6 +130,9 @@
     own_z,
     stress_x,
     part_x,
+    arrived,
+    scale,
+    rank,
     flat_a,
     flat_b,
     send_x,
@@ -295,14 +299,22 @@
     center = (upper_edge + lower_edge) / 2.0
     radius = (upper_edge - lower_edge) / 2.0
     sigma_ratio = center / radius
+    none_row = jnp.zeros((1, 128), jnp.float32)
+    one_row = jnp.ones((1, 128), jnp.float32)
+    coef[0, 0] = none_row
+    coef[1, 0] = none_row
+    coef[2, 0] = one_row
     for sweep in range(SWEEPS):
-        coef[0, sweep * CHEB] = jnp.zeros((1, 128), jnp.float32)
-        coef[1, sweep * CHEB] = 1.0 / center
+        first = sweep * CHEB + 1
+        coef[0, first] = none_row
+        coef[1, first] = 1.0 / center
+        coef[2, first] = none_row
         factor = 1.0 / sigma_ratio
         for later in range(1, CHEB):
             factor_next = 1.0 / (2.0 * sigma_ratio - factor)
-            coef[0, sweep * CHEB + later] = factor_next * factor
-            coef[1, sweep * CHEB + later] = 2.0 * factor_next / radius
+            coef[0, first + later] = factor_next * factor
+            coef[1, first + later] = 2.0 * factor_next / radius
+            coef[2, first + later] = none_row
             factor = factor_next
 
     kinds = jnp.concatenate([material[:, b, :] for b in range(elems_y)], axis=0)
@@ -338,7 +350,7 @@
 
     for c in range(3):
         local_sum(inverse, c)
-        post(inverse, 1, c)
+        post(inverse, 2, c)
 
     weights, derivative, _, own, second = element_tables()
     edge = float(np.float32(1.0 / weights[0]))
@@ -349,6 +361,12 @@
             jnp.concatenate(parts, axis=1), matrix[...], preferred_element_type=jnp.float32
         )
         return (both[:, :128] + both[:, 128:]).reshape(full)
+
+    def joint(parts, matrix):
+        both = jnp.dot(
+            jnp.concatenate(parts, axis=1), matrix[...], preferred_element_type=jnp.float32
+        )
+        return (both[:, :128] + both[:, 128:]).reshape(2, N1, cols, 128)
 
     def forward(c, j, values):
         if c == 2:
@@ -358,11 +376,6 @@
             outs = apply_pairs(own, lines, -1) if c == 0 else apply_pairs(second, lines, 1)
             for i in range(N1):
                 along_x[c, i, j, rows] = outs[i]
-
-    def begin(c):
-        @pl.loop(0, N1, unroll=N1)
-        def _(j):
-            forward(c, j, field[c, :, j])
 
     def advance(c, step):
         alpha = coef[0, step]
@@ -454,7 +467,10 @@
         parts = halves(stacked(lines_x)) + halves(stacked(lines_v))
         resid[0, :, j] = source[0, :, j] - product(parts, second_mat)
 
-    def residuals(slot):
+    def volume(step):
+        for c in (1, 2, 0):
+            advance(c, step)
+
         @pl.loop(1, DEG, unroll=UNROLL)
         def _(i):
             sheet(i, None)
@@ -462,50 +478,222 @@
         for side in range(2):
             sheet(side * DEG, edge if side else -edge)
 
-        @pl.loop(1, 3)
-        def _(c):
-            local_sum(resid, c)
-            post(resid, slot, c)
-
         @pl.loop(0, N1, unroll=N1)
         def _(j):
             closing(j)
 
-        local_sum(resid, 0)
-        post(resid, slot, 0)
+    row_id = lax.broadcasted_iota(jnp.int32, (cols, 128), 0)
+    col_x = row_id % elems_x
+    low_side = (col_x == 0, row_id < elems_x)
+    high_side = (col_x == last_x, row_id >= last_y)
+
+    def by_side(axis, low, high):
+        zero = jnp.zeros((cols, 128), jnp.float32)
+        return jnp.where(low_side[axis], low, jnp.where(high_side[axis], high, zero))
+
+    def rank_tables():
+        for axis in range(2):
+            for p in range(N1):
+                rows = []
+                for f in (0, DEG):
+                    others = [k for k in range(N1) if k != f]
+                    chain = sum(derivative[k, p] * weights[k] * own[k, f] for k in others)
+                    away = 0.0 if p == f else weights[p]
+                    rows.append((derivative[f, p], -chain, away * second[p, f], away * own[p, f]))
+                for kind in range(4):
+                    low, high = (float(np.float32(row[kind])) for row in rows)
+                    rank[axis, kind, p] = by_side(axis, low, high)
+
+    def spot(ref, axis, c, p, t):
+        return ref.at[c, p, t] if axis == 0 else ref.at[c, t, p]
+
+    def face_scales():
+        for axis in range(2):
+            for c in range(3):
+                for t in range(N1):
+                    scale[axis, c, t] = by_side(
+                        axis, spot(inverse, axis, c, 0, t)[...], spot(inverse, axis, c, DEG, t)[...]
+                    )
+
+    def wait_for(slot, kinds):
+        for c in range(3):
+            made = copies(slot, c)
+            for d in kinds:
+                made[d].wait()
+
+    def arrive_y(slot):
+        for c in range(3):
+            arrived[1, c, :, 0:elems_x, :] = recv_y[slot, c, 0]
+            arrived[1, c, :, last_y:cols, :] = recv_y[slot, c, 1]
+
+    def arrive_x(slot):
+        for c in range(3):
+            for b in range(elems_y):
+                at = b * elems_x
+                arrived[0, c, :, at : at + 1, :] = recv_x[slot, c, 0, :, b : b + 1, :]
+                at = b * elems_x + last_x
+                arrived[0, c, :, at : at + 1, :] = recv_x[slot, c, 1, :, b : b + 1, :]
+            for a in range(2):
+                for b in range(2):
+                    at = a * last_x + b * last_y
+                    arrived[0, c, b * DEG, at : at + 1, :] += (
+                        recv_c[slot, c, 2 * a + b] + recv_y[slot, c, b, a * DEG, a * last_x : a * last_x + 1, :]
+                    )
+
+    def correct(axis, step):
+        normal, side = axis, 1 - axis
+        beta = coef[1, step]
+        plain = coef[2, step]
+        edge_z = edge_in[...]
+        edge_n = by_side(axis, -edge, edge)
+        own_f = by_side(axis, float(np.float32(own[0, 0])), float(np.float32(own[DEG, DEG])))
+        second_f = float(np.float32(second[0, 0]))
+        per_w = float(np.float32(1.0 / weights[0]))
+        d = [[None] * N1 for _ in range(3)]
+        for c in range(3):
+            for t in range(N1):
+                value = (plain + beta * scale[axis, c, t]) * arrived[axis, c, t]
+                value = jnp.where(low_side[axis] | high_side[axis], value, 0.0)
+                if axis == 1 and t in (0, DEG):
+                    value = jnp.where(col_x == (0 if t == 0 else last_x), 0.0, value)
+                d[c][t] = value
+                at_low = jnp.where(low_side[axis], value, 0.0)
+                at_high = jnp.where(high_side[axis], value, 0.0)
+                for ref in (field, change):
+                    low = spot(ref, axis, c, 0, t)
+                    high = spot(ref, axis, c, DEG, t)
+                    low[...] = low[...] + at_low
+                    high[...] = high[...] + at_high
+        d_n, d_t, d_z = d[normal], d[side], d[2]
+
+        def stack(lines):
+            return jnp.concatenate(lines, axis=0)
+
+        g_z = product(halves(stack(d_z)), own_mat)
+        g_t = apply_pairs(own, d_t, -1)
+        second_n = apply_pairs(second, d_n, 1)
+        second_z = apply_pairs(second, d_z, 1)
+        t_n, t_t, t_z, left, v_n, v_t, extra, f_z = [[] for _ in range(8)]
+        stiff, mixed, mixed_t, mixed_z, one_t, one_z = [[] for _ in range(6)]
+        for t in range(N1):
+            lam = lam_w[0, t]
+            mu = mu_w[0, t]
+            g_n = own_f * d_n[t]
+            g_nt = g_n + g_t[t]
+            total = g_nt + g_z[t]
+            e_n = edge_n * d_n[t]
+            e_z = edge_z * d_z[t]
+            div = (e_n + e_z) - total
+            own_t = g_t[t]
+            right = second_f * d_t[t]
+            lam_in = per_w * lam
+            mu_in = per_w * mu
+            mu_d = mu_in * d_n[t]
+            mixed.append((lam_in + mu_in) * d_n[t])
+            stiff.append(mixed[t] + mu_d)
+            if t in (0, DEG):
+                edge_t = -edge if t == 0 else edge
+                e_t = edge_t * d_t[t]
+                div = div + e_t
+                own_t = own_t - (e_t + e_t)
+                right = right + edge_t * (g_n + g_z[t])
+                mixed_t.append(edge_t * mu_d)
+            else:
+                mixed_t.append(None)
+            base = lam * div - mu * total
+            t_n.append(base + mu * ((e_n + e_n) - g_n))
+            t_t.append(base - mu * own_t)
+            t_z.append(base + mu * ((e_z + e_z) - g_z[t]))
+            left.append(mu * (second_n[t] + edge_n * (g_t[t] + g_z[t])))
+            v_n.append(mu * d_n[t])
+            v_t.append(mu * d_t[t])
+            extra.append(mu * right)
+            f_z.append(mu * ((second_f * d_z[t] + second_z[t]) + edge_z * g_nt))
+            mixed_z.append(edge_z * mu_d)
+            one_t.append(mu_in * d_t[t])
+            one_z.append(mu_in * d_z[t])
+        back_t = apply_pairs(derivative.T, t_t, -1)
+        back_m = apply_pairs(-derivative.T, mixed, -1)
+        f_t = [back_t[t] + extra[t] for t in range(N1)]
+        two_t = [back_m[t] if mixed_t[t] is None else back_m[t] + mixed_t[t] for t in range(N1)]
+        minus = [-m for m in mixed]
+        joined = jnp.dot(
+            jnp.concatenate(halves(stack(t_n + stiff + one_t + two_t + one_z)), axis=1),
+            exact_mat[...],
+            preferred_element_type=jnp.float32,
+        ).reshape(5, N1, cols, 128)
+        parts = halves(stack(left + f_t)) + halves(stack(v_n + v_t))
+        faces = joint(parts, second_mat)
+        parts = halves(stack(f_z + mixed_z)) + halves(stack(t_z + minus))
+        upright = joint(parts, back_mat)
+        at_face = {normal: faces[0], side: faces[1], 2: upright[0]}
+        pairs = {
+            normal: (0, joined[0], joined[1]),
+            side: (2, joined[2], joined[3]),
+            2: (2, joined[4], upright[1]),
+        }
+        for t in range(N1):
+            for c in range(3):
+                kind, first, second_part = pairs[c]
+                for p in range(N1):
+                    value = rank[axis, kind, p] * first[t] + rank[axis, kind + 1, p] * second_part[t]
+                    if p == 0:
+                        value = value + jnp.where(low_side[axis], at_face[c][t], 0.0)
+                    if p == DEG:
+                        value = value + jnp.where(high_side[axis], at_face[c][t], 0.0)
+                    place = spot(resid, axis, c, p, t)
+                    place[...] = place[...] - value
 
     @pl.loop(0, 3)
     def _(c):
         enter(source_in, source, c)
 
-    for c in (1, 2, 0):
-        collect(field, 0, c)
-        begin(c)
-
-    @pl.loop(0, 3)
-    def _(c):
-        collect(inverse, 1, c)
-
-        @pl.loop(0, N1)
-        def _(i):
-            inverse[c, i] = 1.0 / inverse[c, i]
-            change[c, i] = zeros_big
-
-    @pl.loop(0, steps)
+    rank_tables()
+
+    @pl.loop(0, 2 * 3 * N1)
+    def _(at):
+        arrived[at // (3 * N1), (at // N1) % 3, at % N1] = jnp.zeros((cols, 128), jnp.float32)
+        scale[at // (3 * N1), (at // N1) % 3, at % N1] = jnp.zeros((cols, 128), jnp.float32)
+
+    @pl.loop(0, 3 * N1)
+    def _(at):
+        change[at // N1, at % N1] = zeros_big
+        resid[at // N1, at % N1] = zeros_big
+
+    @pl.loop(0, steps + 1)
     def _(step):
-        slot = 2 + step % 2
-        residuals(slot)
-
-        for c in (1, 2, 0):
-            collect(resid, slot, c)
-            advance(c, step)
-
-    slot = 2 + steps % 2
-    residuals(slot)
+        volume(step)
+
+        slot = step % 2
+        wait_for(slot, (2, 3))
+        arrive_y(slot)
+        correct(1, step)
+        wait_for(slot, (0, 1, 4, 5, 6, 7))
+        arrive_x(slot)
+        correct(0, step)
+
+        @pl.loop(0, 3)
+        def _(c):
+            local_sum(resid, c)
+            post(resid, 1 - slot, c)
+
+        @pl.when(step == 0)
+        def _():
+            @pl.loop(0, 3)
+            def _(c):
+                collect(inverse, 2, c)
+
+                @pl.loop(0, N1)
+                def _(i):
+                    inverse[c, i] = 1.0 / inverse[c, i]
+
+            face_scales()
 
     @pl.loop(0, 3)
     def _(c):
         leave(field, smoothed_out, c)
+
+    slot = (steps + 1) % 2
 
     @pl.loop(0, 3)
     def _(c):
@@ -546,6 +734,7 @@
     back_mat = jnp.asarray(np.block(exact_join + exact_pair(back_np)))
     scaled_np = np.kron(eye_z, second_np) @ join_np
     second_mat = jnp.asarray(np.block(exact_join + exact_pair(scaled_np)))
+    exact_mat = jnp.asarray(np.concatenate([joined, joined], axis=0))
     edge_np = np.zeros((1, lanes))
     edge_np[0, 0::N1] = -1.0 / weights_np[0]
     edge_np[0, DEG::N1] = 1.0 / weights_np[DEG]
@@ -583,6 +772,7 @@
     smem = pl.BlockSpec(memory_space=pltpu.SMEM)
     big = pltpu.VMEM(whole, jnp.float32)
     small = pltpu.VMEM((N1, N1, cols, lanes), jnp.float32)
+    face = pltpu.VMEM((2, 3, N1, cols, lanes), jnp.float32)
     lines = pltpu.VMEM((DEG * elems_y, pad_x, lanes), jnp.float32)
     face_x = pltpu.VMEM((SLOTS, 3, 2, N1, elems_y, lanes), jnp.float32)
     face_y = pltpu.VMEM((SLOTS, 3, 2, N1, elems_x, lanes), jnp.float32)
@@ -595,13 +785,15 @@
     return pl.pallas_call(
         kernel,
         out_shape=(shape, shape),
-        in_specs=[smem] * 3 + [vmem] * 14,
+        in_specs=[smem] * 3 + [vmem] * 15,
         out_specs=(vmem, vmem),
-        scratch_shapes=[pltpu.VMEM((2, SWEEPS * CHEB, 1, lanes), jnp.float32)]
+        scratch_shapes=[pltpu.VMEM((3, SWEEPS * CHEB + 1, 1, lanes), jnp.float32)]
         + [big] * 3
         + [small] * 2
         + [big] * 3
         + [small] * 3
+        + [face] * 2
+        + [pltpu.VMEM((2, 4, N1, cols, lanes), jnp.float32)]
         + [lines] * 2
         + [face_x, face_y, corner] * 2
         + [pltpu.SemaphoreType.DMA((SLOTS, 3, 8))] * 2,
@@ -623,6 +815,7 @@
         own_mat,
         back_mat,
         second_mat,
+        exact_mat,
         join_in,
     )
 

time: 75.6 us -> 66.8 us (0.88)
  Pallas kernels: 69.9 us -> 61 us
    pallas_call x1, Pallas kernels: 69.9 us -> 61 us  [local(): pl.pallas_call(kernel, out_shape=(shape, shape), in_specs=[smem] * 3 + [v...]
where the time goes in v2:
time: 66.8 us; the launch traced here: 66.5 us
  Pallas kernels  61 us (91%)
  local copies, waits for them, and re-layouts  3.53 us (5%)
  between operations  1.94 us (3%)
    pallas_call x1, Pallas kernels, local(): pl.pallas_call(kernel, out_shape=(shape, shape), in_specs=[smem] * 3 + [v...  61 us
    unnamed x4, local copies, waits for them, and re-layouts  3.53 us

profile of v2, /device:TPU:0, one launch (start us, length us, event | category | flops | bytes accessed | tf_op | source)
XLA Modules:
  0.0 66.5 jit_solution(3641482730179148783)
XLA Ops:
  1.9 61.0 %shard_map.185 = (f32[3,28,3108]{2,1,0:T(8,128)}, f32[3,28,3108]{2,1,0:T(8,128)}) custom-call(f32[2,8]{1,0:T(2,128)} %refs_0_.1, f32[1]{0:T(128)S(6)} %copy.22.refs_1_, f32[1]{0:T(128)S(6)} %copy.23.refs_2_, f32[3,28,3108]{2,1,0:T(8,128)} %refs_3_.1, f32[3,28,3108]{2,1,0:T(8,128)} %refs_4_.1, s32[4,4,16]{2,1,0:T(4,128)} %refs_5_.1, ...), custom_call_target="tpu_custom_call" | custom-call | tf_op jit(solution)/shard_map/pallas_call | solution.py:785
  62.9 0.0 copy-start
  62.9 2.5 %copy.24 = f32[3,28,3108]{2,1,0:T(8,128)} copy(f32[3,28,3108]{2,1,0:T(8,128)} %get-tuple-element.4) | data formatting | bytes 2088576
  65.4 0.0 copy-done
  65.4 1.0 %copy.25 = f32[3,28,3108]{2,1,0:T(8,128)} copy(f32[3,28,3108]{2,1,0:T(8,128)S(1)} %copy-done) | data formatting | bytes 2088576
Async XLA Ops:
  62.9 2.5 %copy-start = (f32[3,28,3108]{2,1,0:T(8,128)S(1)}, f32[3,28,3108]{2,1,0:T(8,128)}, u32[]{:S(2)}) copy-start(f32[3,28,3108]{2,1,0:T(8,128)} %get-tuple-element.5) | copy-start | bytes 3132868

commit v3 on v2

--- a/solution.py
+++ b/solution.py
@@ -94,6 +94,42 @@
     return weights, derivative, ratio, own, second
 
 
+class Loads:
+    def __init__(self, places, staged, part_sem, whole_sem, put_sem):
+        self.places = places
+        self.staged = staged
+        self.part_sem = part_sem
+        self.whole_sem = whole_sem
+        self.put_sem = put_sem
+
+    def part(self, at, c):
+        return pltpu.make_async_copy(
+            self.places[at].at[c], self.staged[at].at[c], self.part_sem.at[at, c]
+        )
+
+    def whole(self, at):
+        return pltpu.make_async_copy(self.places[at], self.staged[at], self.whole_sem.at[at])
+
+    def put(self, at, out, c):
+        return pltpu.make_async_copy(self.staged[at].at[c], out.at[c], self.put_sem.at[at, c])
+
+    def start(self):
+        self.whole(7).start()
+        for c in range(3):
+            self.part(0, c).start()
+        for at in range(2, len(self.places)):
+            if at != 7:
+                self.whole(at).start()
+        for c in range(3):
+            self.part(1, c).start()
+
+    def wait_part(self, at, c):
+        self.part(at, c).wait()
+
+    def wait_whole(self, at):
+        self.whole(at).wait()
+
+
 def smoother_kernel(
     steps,
     elems_x,
@@ -101,21 +137,7 @@
     lame,
     upper,
     lower_ratio,
-    guess_in,
-    source_in,
-    material,
-    weight_in,
-    own_in,
-    sum_in,
-    spread_in,
-    gather_in,
-    select_in,
-    edge_in,
-    own_mat,
-    back_mat,
-    second_mat,
-    exact_mat,
-    join_in,
+    loads,
     smoothed_out,
     residual_out,
     coef,
@@ -130,9 +152,18 @@
     own_z,
     stress_x,
     part_x,
-    arrived,
-    scale,
-    rank,
+    arrived_x,
+    arrived_y,
+    scale_x,
+    scale_y,
+    rank_x,
+    rank_y,
+    rim,
+    delta,
+    narrow,
+    wide,
+    face_w,
+    edge_lines,
     flat_a,
     flat_b,
     send_x,
@@ -144,6 +175,9 @@
     send_sem,
     recv_sem,
 ):
+    loads.start()
+    (guess_in, source_in, material, weight_in, own_in, sum_in, spread_in, gather_in) = loads.staged[:8]
+    (select_in, edge_in, own_mat, back_mat, second_mat, exact_mat, join_in) = loads.staged[8:]
     cols = elems_x * elems_y
     size_x = lax.axis_size("gx")
     size_y = lax.axis_size("gy")
@@ -160,27 +194,34 @@
             barrier, inc=1, device_id=partner, device_id_type=pl.DeviceIdType.MESH
         )
 
-    def copies(slot, c):
-        made = []
-        for d in range(8):
-            if d < 2:
-                src, dst = send_x.at[slot, c, d], recv_x.at[slot, c, 1 - d]
-            elif d < 4:
-                src, dst = send_y.at[slot, c, d - 2], recv_y.at[slot, c, 3 - d]
-            else:
-                src, dst = send_c.at[slot, c, d - 4], recv_c.at[slot, c, 7 - d]
-            mirror = (1, 0, 3, 2, 7, 6, 5, 4)[d]
-            made.append(
-                pltpu.make_async_remote_copy(
-                    src_ref=src,
-                    dst_ref=dst,
-                    send_sem=send_sem.at[slot, c, d],
-                    recv_sem=recv_sem.at[slot, c, mirror],
-                    device_id=partners[d],
-                    device_id_type=pl.DeviceIdType.MESH,
-                )
-            )
-        return made
+    def copy_of(slot, d):
+        if d < 2:
+            src, dst = send_x.at[slot, d], recv_x.at[slot, 1 - d]
+        elif d < 4:
+            src, dst = send_y.at[slot, d - 2], recv_y.at[slot, 3 - d]
+        else:
+            src, dst = send_c.at[slot, d - 4], recv_c.at[slot, 7 - d]
+        mirror = (1, 0, 3, 2, 7, 6, 5, 4)[d]
+        return pltpu.make_async_remote_copy(
+            src_ref=src,
+            dst_ref=dst,
+            send_sem=send_sem.at[slot, d],
+            recv_sem=recv_sem.at[slot, mirror],
+            device_id=partners[d],
+            device_id_type=pl.DeviceIdType.MESH,
+        )
+
+    def start_all(slot, kinds):
+        for d in kinds:
+            copy_of(slot, d).start()
+
+    def wait_for(slot, kinds):
+        for d in kinds:
+            copy_of(slot, d).wait()
+
+    along_y = (2, 3)
+    along_x_or_corner = (0, 1, 4, 5, 6, 7)
+    every = range(8)
 
     rows = lax.broadcasted_iota(jnp.int32, (N1 * cols, 128), 0) % cols
     row_x = rows % elems_x
@@ -208,35 +249,34 @@
         ref[c, :, 0] = (low + to_low).reshape(full)
         ref[c, :, DEG] = (high + to_high).reshape(full)
 
-    def post(ref, slot, c):
-        send_y[slot, c, 0] = ref[c, :, 0, 0:elems_x, :]
-        send_y[slot, c, 1] = ref[c, :, DEG, last_y:cols, :]
+    def fill_y(ref, slot, c):
+        send_y[slot, 0, c] = ref[c, :, 0, 0:elems_x, :]
+        send_y[slot, 1, c] = ref[c, :, DEG, last_y:cols, :]
+
+    def fill(ref, slot, c):
+        fill_y(ref, slot, c)
         for b in range(elems_y):
             at = b * elems_x
-            send_x[slot, c, 0, :, b : b + 1, :] = ref[c, 0, :, at : at + 1, :]
+            send_x[slot, 0, c, :, b : b + 1, :] = ref[c, 0, :, at : at + 1, :]
             at = b * elems_x + last_x
-            send_x[slot, c, 1, :, b : b + 1, :] = ref[c, DEG, :, at : at + 1, :]
+            send_x[slot, 1, c, :, b : b + 1, :] = ref[c, DEG, :, at : at + 1, :]
         for a in range(2):
             for b in range(2):
                 at = a * last_x + b * last_y
-                send_c[slot, c, 2 * a + b] = ref[c, a * DEG, b * DEG, at : at + 1, :]
-        for copy in copies(slot, c):
-            copy.start()
+                send_c[slot, 2 * a + b, c] = ref[c, a * DEG, b * DEG, at : at + 1, :]
 
     def collect(ref, slot, c):
-        for copy in copies(slot, c):
-            copy.wait()
-        ref[c, :, 0, 0:elems_x, :] += recv_y[slot, c, 0]
-        ref[c, :, DEG, last_y:cols, :] += recv_y[slot, c, 1]
+        ref[c, :, 0, 0:elems_x, :] += recv_y[slot, 0, c]
+        ref[c, :, DEG, last_y:cols, :] += recv_y[slot, 1, c]
         for b in range(elems_y):
             at = b * elems_x
-            ref[c, 0, :, at : at + 1, :] += recv_x[slot, c, 0, :, b : b + 1, :]
+            ref[c, 0, :, at : at + 1, :] += recv_x[slot, 0, c, :, b : b + 1, :]
             at = b * elems_x + last_x
-            ref[c, DEG, :, at : at + 1, :] += recv_x[slot, c, 1, :, b : b + 1, :]
+            ref[c, DEG, :, at : at + 1, :] += recv_x[slot, 1, c, :, b : b + 1, :]
         for a in range(2):
             for b in range(2):
                 at = a * last_x + b * last_y
-                ref[c, a * DEG, b * DEG, at : at + 1, :] += recv_c[slot, c, 2 * a + b]
+                ref[c, a * DEG, b * DEG, at : at + 1, :] += recv_c[slot, 2 * a + b, c]
 
     nodes_x = DEG * elems_x
     nodes_y = DEG * elems_y
@@ -283,17 +323,18 @@
         lines = [flat_a[y, 0:nodes_x, 0:nodes_z] for y in range(nodes_y)]
         flat_out[c] = jnp.concatenate(lines, axis=1)
 
+    loads.wait_whole(7)
+
     @pl.loop(0, 3)
     def _(c):
+        loads.wait_part(0, c)
         enter(guess_in, field, c)
         local_sum(field, c)
 
-    pl.semaphore_wait(barrier, len(partners))
-
-    @pl.loop(0, 3)
-    def _(c):
-        post(field, 0, c)
-
+
+    for at in range(2, len(loads.staged)):
+        if at != 7:
+            loads.wait_whole(at)
     upper_edge = jnp.full((1, 128), upper[0], jnp.float32)
     lower_edge = lower_ratio[0] * upper_edge
     center = (upper_edge + lower_edge) / 2.0
@@ -350,7 +391,6 @@
 
     for c in range(3):
         local_sum(inverse, c)
-        post(inverse, 2, c)
 
     weights, derivative, _, own, second = element_tables()
     edge = float(np.float32(1.0 / weights[0]))
@@ -361,12 +401,6 @@
             jnp.concatenate(parts, axis=1), matrix[...], preferred_element_type=jnp.float32
         )
         return (both[:, :128] + both[:, 128:]).reshape(full)
-
-    def joint(parts, matrix):
-        both = jnp.dot(
-            jnp.concatenate(parts, axis=1), matrix[...], preferred_element_type=jnp.float32
-        )
-        return (both[:, :128] + both[:, 128:]).reshape(2, N1, cols, 128)
 
     def forward(c, j, values):
         if c == 2:
@@ -413,33 +447,33 @@
                 g_x = along_x[0, i, j, rows]
                 g_z = own_z[i, j, rows]
                 g_xy = g_x + g_y[j]
-                total = g_xy + g_z
                 e_z = edge_z * u_z[j]
-                div = e_z - total
-                own_x = -g_x
-                own_y = -g_y[j]
+                away_z = g_z - e_z
+                shrink = g_xy + away_z
+                own_x = g_x
+                own_y = g_y[j]
                 left = second_x[j]
                 right = along_x[1, i, j, rows]
                 if edge_x is not None:
                     e_x = edge_x * u_x[j]
-                    div = div + e_x
-                    own_x = (e_x + e_x) - g_x
+                    shrink = shrink - e_x
+                    own_x = g_x - (e_x + e_x)
                     left = left + edge_x * (g_y[j] + g_z)
                 if j in (0, DEG):
                     edge_y = -edge if j == 0 else edge
                     e_y = edge_y * u_y[j]
-                    div = div + e_y
-                    own_y = (e_y + e_y) - g_y[j]
+                    shrink = shrink - e_y
+                    own_y = g_y[j] - (e_y + e_y)
                     right = right + edge_y * (g_x + g_z)
-                base = lam * div - mu * total
+                base = lam * shrink + mu * (g_xy + g_z)
                 stress_x[i, j, rows] = base + mu * own_x
                 part_x[i, j, rows] = mu * left
                 t_y.append(base + mu * own_y)
                 extra_y.append(mu * right)
                 group_v.append(mu * u_y[j])
-                group_t.append(base + mu * ((e_z + e_z) - g_z))
+                group_t.append(base + mu * (away_z - e_z))
                 group_z.append(mu * ((along_x[2, i, j, rows] + second_z[j]) + edge_z * g_xy))
-            back_y = apply_pairs(derivative.T, t_y, -1)
+            back_y = apply_pairs(-derivative.T, t_y, -1)
             lines_y.append([back_y[j] + extra_y[j] for j in range(N1)])
             lines_v.append(group_v)
             lines_z.append(group_z)
@@ -457,7 +491,7 @@
         lines_x = []
         lines_v = []
         for rows in groups:
-            back_x = apply_pairs(derivative.T, [stress_x[i, j, rows] for i in range(N1)], -1)
+            back_x = apply_pairs(-derivative.T, [stress_x[i, j, rows] for i in range(N1)], -1)
             lines_x.append([part_x[i, j, rows] + back_x[i] for i in range(N1)])
             lines_v.append([mu_w[i, j, rows] * field[0, i, j, rows] for i in range(N1)])
 
@@ -467,7 +501,7 @@
         parts = halves(stacked(lines_x)) + halves(stacked(lines_v))
         resid[0, :, j] = source[0, :, j] - product(parts, second_mat)
 
-    def volume(step):
+    def volume(step, slot):
         for c in (1, 2, 0):
             advance(c, step)
 
@@ -478,18 +512,26 @@
         for side in range(2):
             sheet(side * DEG, edge if side else -edge)
 
+        wait_for(slot, along_y)
+
         @pl.loop(0, N1, unroll=N1)
         def _(j):
             closing(j)
 
+    arrived = (arrived_x, arrived_y)
+    scale = (scale_x, scale_y)
+    per_side = (elems_y, elems_x)
+    ring = 2 * elems_x
+    windows = (slice(0, ring), slice(cols - ring, cols))
     row_id = lax.broadcasted_iota(jnp.int32, (cols, 128), 0)
-    col_x = row_id % elems_x
-    low_side = (col_x == 0, row_id < elems_x)
-    high_side = (col_x == last_x, row_id >= last_y)
+    ring_id = [lax.broadcasted_iota(jnp.int32, (2 * size, 128), 0) for size in per_side]
+    low_side = [ring_id[axis] < per_side[axis] for axis in range(2)]
+    place_t = [ring_id[axis] % per_side[axis] for axis in range(2)]
+    lines_low = pl.ds(0, elems_y, stride=elems_x)
+    lines_high = pl.ds(last_x, elems_y, stride=elems_x)
 
     def by_side(axis, low, high):
-        zero = jnp.zeros((cols, 128), jnp.float32)
-        return jnp.where(low_side[axis], low, jnp.where(high_side[axis], high, zero))
+        return jnp.where(low_side[axis], low, high)
 
     def rank_tables():
         for axis in range(2):
@@ -498,49 +540,83 @@
                 for f in (0, DEG):
                     others = [k for k in range(N1) if k != f]
                     chain = sum(derivative[k, p] * weights[k] * own[k, f] for k in others)
-                    away = 0.0 if p == f else weights[p]
-                    rows.append((derivative[f, p], -chain, away * second[p, f], away * own[p, f]))
+                    away = float(p != f)
+                    heavy = away * weights[p]
+                    rows.append((away * derivative[f, p], -away * chain, heavy * second[p, f], heavy * own[p, f]))
                 for kind in range(4):
                     low, high = (float(np.float32(row[kind])) for row in rows)
-                    rank[axis, kind, p] = by_side(axis, low, high)
-
-    def spot(ref, axis, c, p, t):
-        return ref.at[c, p, t] if axis == 0 else ref.at[c, t, p]
+                    if axis == 0:
+                        col = row_id % elems_x
+                        rank_x[kind, p] = jnp.where(col == 0, low, jnp.where(col == last_x, high, 0.0))
+                    else:
+                        rank_y[0, kind, p] = by_side(1, low, 0.0)
+                        rank_y[1, kind, p] = by_side(1, 0.0, high)
+
+    def gather_x(ref, c, low, high, dst, at):
+        half = per_side[0]
+        for t in range(N1):
+            dst[at, t, 0:half, :] = ref[c, low, t, lines_low, :]
+            dst[at, t, half : 2 * half, :] = ref[c, high, t, lines_high, :]
+
+    def face_y(ref, c, t):
+        return jnp.where(low_side[1], ref[c, t, 0, windows[0]], ref[c, t, DEG, windows[1]])
+
+    def add_y(ref, c, t, value):
+        ref[c, t, 0, windows[0]] = ref[c, t, 0, windows[0]] + by_side(1, value, 0.0)
+        ref[c, t, DEG, windows[1]] = ref[c, t, DEG, windows[1]] + by_side(1, 0.0, value)
+
+    def add_x(ref, c, t):
+        half = per_side[0]
+        ref[c, 0, t, lines_low, :] = ref[c, 0, t, lines_low, :] + delta[c, t, 0:half, :]
+        ref[c, DEG, t, lines_high, :] = ref[c, DEG, t, lines_high, :] + delta[c, t, half : 2 * half, :]
+
+    def face_weights():
+        half = per_side[0]
+        for kind, ref in enumerate((lam_w, mu_w)):
+            for t in range(N1):
+                face_w[0, kind, t, 0:half, :] = ref[0, t, lines_low, :]
+                face_w[0, kind, t, half : 2 * half, :] = ref[0, t, lines_high, :]
+                face_w[1, kind, t] = jnp.where(low_side[1], ref[0, t, windows[0]], ref[0, t, windows[1]])
 
     def face_scales():
-        for axis in range(2):
-            for c in range(3):
-                for t in range(N1):
-                    scale[axis, c, t] = by_side(
-                        axis, spot(inverse, axis, c, 0, t)[...], spot(inverse, axis, c, DEG, t)[...]
-                    )
-
-    def wait_for(slot, kinds):
         for c in range(3):
-            made = copies(slot, c)
-            for d in kinds:
-                made[d].wait()
+            gather_x(inverse, c, 0, DEG, scale_x, c)
+            for t in range(N1):
+                scale_y[c, t] = face_y(inverse, c, t)
 
     def arrive_y(slot):
         for c in range(3):
-            arrived[1, c, :, 0:elems_x, :] = recv_y[slot, c, 0]
-            arrived[1, c, :, last_y:cols, :] = recv_y[slot, c, 1]
+            arrived_y[c, :, 0:elems_x, :] = recv_y[slot, 0, c]
+            arrived_y[c, :, elems_x:ring, :] = recv_y[slot, 1, c]
 
     def arrive_x(slot):
+        half = per_side[0]
         for c in range(3):
-            for b in range(elems_y):
-                at = b * elems_x
-                arrived[0, c, :, at : at + 1, :] = recv_x[slot, c, 0, :, b : b + 1, :]
-                at = b * elems_x + last_x
-                arrived[0, c, :, at : at + 1, :] = recv_x[slot, c, 1, :, b : b + 1, :]
+            arrived_x[c, :, 0:half, :] = recv_x[slot, 0, c]
+            arrived_x[c, :, half : 2 * half, :] = recv_x[slot, 1, c]
             for a in range(2):
                 for b in range(2):
-                    at = a * last_x + b * last_y
-                    arrived[0, c, b * DEG, at : at + 1, :] += (
-                        recv_c[slot, c, 2 * a + b] + recv_y[slot, c, b, a * DEG, a * last_x : a * last_x + 1, :]
+                    at = a * half + b * (half - 1)
+                    arrived_x[c, b * DEG, at : at + 1, :] += (
+                        recv_c[slot, 2 * a + b, c] + recv_y[slot, b, c, a * DEG, a * last_x : a * last_x + 1, :]
                     )
 
-    def correct(axis, step):
+    def send_rim(slot):
+        half = per_side[0]
+        for c in range(3):
+            low = rim[c, 0]
+            high = rim[c, DEG]
+            rim[c, 0] = low + jnp.where(place_t[0] >= 1, pltpu.roll(high, 1, 0), 0.0)
+            rim[c, DEG] = high + jnp.where(place_t[0] < half - 1, pltpu.roll(low, 2 * half - 1, 0), 0.0)
+            send_x[slot, 0, c] = rim[c, :, 0:half, :]
+            send_x[slot, 1, c] = rim[c, :, half : 2 * half, :]
+            for a in range(2):
+                for b in range(2):
+                    at = a * half + b * (half - 1)
+                    send_c[slot, 2 * a + b, c] = rim[c, b * DEG, at : at + 1, :]
+        start_all(slot, along_x_or_corner)
+
+    def correct(axis, step, slot):
         normal, side = axis, 1 - axis
         beta = coef[1, step]
         plain = coef[2, step]
@@ -549,136 +625,187 @@
         own_f = by_side(axis, float(np.float32(own[0, 0])), float(np.float32(own[DEG, DEG])))
         second_f = float(np.float32(second[0, 0]))
         per_w = float(np.float32(1.0 / weights[0]))
+        chain_f = [sum(derivative[k, f] * weights[k] * own[k, f] for k in range(N1) if k != f) for f in (0, DEG)]
+        first_f = by_side(axis, float(np.float32(derivative[0, 0])), float(np.float32(derivative[DEG, DEG])))
+        then_f = by_side(axis, *(float(np.float32(-value)) for value in chain_f))
+        size = 2 * per_side[axis]
+        half = per_side[0]
         d = [[None] * N1 for _ in range(3)]
         for c in range(3):
             for t in range(N1):
-                value = (plain + beta * scale[axis, c, t]) * arrived[axis, c, t]
-                value = jnp.where(low_side[axis] | high_side[axis], value, 0.0)
+                value = (plain + beta * scale[axis][c, t]) * arrived[axis][c, t]
                 if axis == 1 and t in (0, DEG):
-                    value = jnp.where(col_x == (0 if t == 0 else last_x), 0.0, value)
+                    value = jnp.where(place_t[1] == (0 if t == 0 else last_x), 0.0, value)
                 d[c][t] = value
-                at_low = jnp.where(low_side[axis], value, 0.0)
-                at_high = jnp.where(high_side[axis], value, 0.0)
-                for ref in (field, change):
-                    low = spot(ref, axis, c, 0, t)
-                    high = spot(ref, axis, c, DEG, t)
-                    low[...] = low[...] + at_low
-                    high[...] = high[...] + at_high
         d_n, d_t, d_z = d[normal], d[side], d[2]
 
         def stack(lines):
             return jnp.concatenate(lines, axis=0)
 
-        g_z = product(halves(stack(d_z)), own_mat)
+        def joint(parts, matrix, count):
+            both = jnp.dot(
+                jnp.concatenate(parts, axis=1), matrix[...], preferred_element_type=jnp.float32
+            )
+            return (both[:, :128] + both[:, 128:]).reshape(count, N1, size, 128)
+
+        g_z = joint(halves(stack(d_z)), own_mat, 1)[0]
         g_t = apply_pairs(own, d_t, -1)
         second_n = apply_pairs(second, d_n, 1)
         second_z = apply_pairs(second, d_z, 1)
         t_n, t_t, t_z, left, v_n, v_t, extra, f_z = [[] for _ in range(8)]
         stiff, mixed, mixed_t, mixed_z, one_t, one_z = [[] for _ in range(6)]
         for t in range(N1):
-            lam = lam_w[0, t]
-            mu = mu_w[0, t]
+            lam = face_w[axis, 0, t]
+            mu = face_w[axis, 1, t]
             g_n = own_f * d_n[t]
             g_nt = g_n + g_t[t]
-            total = g_nt + g_z[t]
             e_n = edge_n * d_n[t]
             e_z = edge_z * d_z[t]
-            div = (e_n + e_z) - total
+            away_z = g_z[t] - e_z
+            shrink = (g_nt + away_z) - e_n
             own_t = g_t[t]
             right = second_f * d_t[t]
-            lam_in = per_w * lam
-            mu_in = per_w * mu
-            mu_d = mu_in * d_n[t]
-            mixed.append((lam_in + mu_in) * d_n[t])
-            stiff.append(mixed[t] + mu_d)
+            mu_d = mu * d_n[t]
+            mu_in = per_w * mu_d
+            mixed.append(per_w * (lam * d_n[t]) + mu_in)
+            stiff.append(mixed[t] + mu_in)
             if t in (0, DEG):
                 edge_t = -edge if t == 0 else edge
                 e_t = edge_t * d_t[t]
-                div = div + e_t
+                shrink = shrink - e_t
                 own_t = own_t - (e_t + e_t)
                 right = right + edge_t * (g_n + g_z[t])
-                mixed_t.append(edge_t * mu_d)
+                mixed_t.append(edge_t * mu_in)
             else:
                 mixed_t.append(None)
-            base = lam * div - mu * total
-            t_n.append(base + mu * ((e_n + e_n) - g_n))
-            t_t.append(base - mu * own_t)
-            t_z.append(base + mu * ((e_z + e_z) - g_z[t]))
+            base = lam * shrink + mu * (g_nt + g_z[t])
+            t_n.append(base + mu * (g_n - (e_n + e_n)))
+            t_t.append(base + mu * own_t)
+            t_z.append(base + mu * (away_z - e_z))
             left.append(mu * (second_n[t] + edge_n * (g_t[t] + g_z[t])))
-            v_n.append(mu * d_n[t])
+            v_n.append(mu_d)
             v_t.append(mu * d_t[t])
             extra.append(mu * right)
             f_z.append(mu * ((second_f * d_z[t] + second_z[t]) + edge_z * g_nt))
-            mixed_z.append(edge_z * mu_d)
-            one_t.append(mu_in * d_t[t])
-            one_z.append(mu_in * d_z[t])
-        back_t = apply_pairs(derivative.T, t_t, -1)
+            mixed_z.append(edge_z * mu_in)
+            one_t.append(per_w * v_t[t])
+            one_z.append(per_w * (mu * d_z[t]))
+        back_t = apply_pairs(-derivative.T, t_t, -1)
         back_m = apply_pairs(-derivative.T, mixed, -1)
         f_t = [back_t[t] + extra[t] for t in range(N1)]
         two_t = [back_m[t] if mixed_t[t] is None else back_m[t] + mixed_t[t] for t in range(N1)]
-        minus = [-m for m in mixed]
-        joined = jnp.dot(
-            jnp.concatenate(halves(stack(t_n + stiff + one_t + two_t + one_z)), axis=1),
-            exact_mat[...],
-            preferred_element_type=jnp.float32,
-        ).reshape(5, N1, cols, 128)
         parts = halves(stack(left + f_t)) + halves(stack(v_n + v_t))
-        faces = joint(parts, second_mat)
-        parts = halves(stack(f_z + mixed_z)) + halves(stack(t_z + minus))
-        upright = joint(parts, back_mat)
-        at_face = {normal: faces[0], side: faces[1], 2: upright[0]}
-        pairs = {
-            normal: (0, joined[0], joined[1]),
-            side: (2, joined[2], joined[3]),
-            2: (2, joined[4], upright[1]),
-        }
+        faces = joint(parts, second_mat, 2)
+        parts = halves(stack(f_z)) + halves(stack(t_z))
+        face_z = joint(parts, back_mat, 1)[0]
+
+        def joined(lines, count):
+            return jnp.dot(
+                jnp.concatenate(halves(stack(lines)), axis=1),
+                exact_mat[...],
+                preferred_element_type=jnp.float32,
+            ).reshape(count, N1, size, 128)
+
+        along_n = joined(t_n + stiff, 2)
+        away = joined(one_t + two_t + one_z, 3)
+        parts = halves(stack(mixed_z)) + halves(stack(mixed))
+        upright = joint(parts, back_mat, 1)[0]
+        at_face = {normal: faces[0], side: faces[1], 2: face_z}
+        if axis == 0:
+            for c in range(3):
+                gather_x(resid, c, 0, DEG, rim, c)
+        for c in range(3):
+            for t in range(N1):
+                value = at_face[c][t]
+                if c == normal:
+                    value = value + (then_f * along_n[1, t] - first_f * along_n[0, t])
+                if axis == 0:
+                    left_over = rim[c, t] - value
+                    rim[c, t] = left_over
+                    delta[c, t] = left_over
+                else:
+                    add_y(resid, c, t, -value)
+        if axis == 0:
+            for c in range(3):
+                for t in range(N1):
+                    resid[c, 0, t, lines_low, :] = delta[c, t, 0:half, :]
+                    resid[c, DEG, t, lines_high, :] = delta[c, t, half : 2 * half, :]
+            send_rim(slot)
+        pairs = {normal: (0, -along_n[0], along_n[1]), side: (2, away[0], away[1]), 2: (2, away[2], upright)}
+        for c in range(3):
+            for t in range(N1):
+                if axis == 0:
+                    delta[c, t] = d[c][t]
+                    add_x(field, c, t)
+                    add_x(change, c, t)
+                else:
+                    add_y(field, c, t, d[c][t])
+                    add_y(change, c, t, d[c][t])
         for t in range(N1):
             for c in range(3):
-                kind, first, second_part = pairs[c]
-                for p in range(N1):
-                    value = rank[axis, kind, p] * first[t] + rank[axis, kind + 1, p] * second_part[t]
-                    if p == 0:
-                        value = value + jnp.where(low_side[axis], at_face[c][t], 0.0)
-                    if p == DEG:
-                        value = value + jnp.where(high_side[axis], at_face[c][t], 0.0)
-                    place = spot(resid, axis, c, p, t)
-                    place[...] = place[...] - value
+                kind, first, then = pairs[c]
+                if axis == 0:
+                    for k, value in enumerate((first[t], then[t])):
+                        narrow[2 * c + k, t] = value
+                        wide[2 * c + k, t, lines_low, :] = narrow[2 * c + k, t, 0:half, :]
+                        wide[2 * c + k, t, lines_high, :] = narrow[2 * c + k, t, half : 2 * half, :]
+                    first_t, then_t = wide[2 * c, t], wide[2 * c + 1, t]
+                    for p in range(N1):
+                        change_by = rank_x[kind, p] * first_t + rank_x[kind + 1, p] * then_t
+                        resid[c, p, t] = resid[c, p, t] - change_by
+                else:
+                    for p in range(N1):
+                        for w, rows in enumerate(windows):
+                            change_by = rank_y[w, kind, p] * first[t] + rank_y[w, kind + 1, p] * then[t]
+                            resid[c, t, p, rows] = resid[c, t, p, rows] - change_by
 
     @pl.loop(0, 3)
     def _(c):
+        loads.wait_part(1, c)
         enter(source_in, source, c)
 
     rank_tables()
-
-    @pl.loop(0, 2 * 3 * N1)
-    def _(at):
-        arrived[at // (3 * N1), (at // N1) % 3, at % N1] = jnp.zeros((cols, 128), jnp.float32)
-        scale[at // (3 * N1), (at // N1) % 3, at % N1] = jnp.zeros((cols, 128), jnp.float32)
-
-    @pl.loop(0, 3 * N1)
-    def _(at):
-        change[at // N1, at % N1] = zeros_big
-        resid[at // N1, at % N1] = zeros_big
+    face_weights()
+    for ref in (scale_x, scale_y, wide):
+        ref[...] = jnp.zeros(ref.shape, jnp.float32)
+
+    for c in range(3):
+
+        @pl.loop(0, N1)
+        def _(i):
+            change[c, i] = zeros_big
+            resid[c, i] = zeros_big
+
+    for c in range(3):
+        fill(field, 0, c)
+        fill(inverse, 2, c)
+
+    pl.semaphore_wait(barrier, len(partners))
+
+    start_all(0, every)
+    start_all(2, every)
 
     @pl.loop(0, steps + 1)
     def _(step):
-        volume(step)
-
         slot = step % 2
-        wait_for(slot, (2, 3))
+        volume(step, slot)
         arrive_y(slot)
-        correct(1, step)
-        wait_for(slot, (0, 1, 4, 5, 6, 7))
+        correct(1, step, 1 - slot)
+        wait_for(slot, along_x_or_corner)
         arrive_x(slot)
-        correct(0, step)
+        correct(0, step, 1 - slot)
 
         @pl.loop(0, 3)
         def _(c):
             local_sum(resid, c)
-            post(resid, 1 - slot, c)
+            fill_y(resid, 1 - slot, c)
+
+        start_all(1 - slot, along_y)
 
         @pl.when(step == 0)
         def _():
+            wait_for(2, every)
+
             @pl.loop(0, 3)
             def _(c):
                 collect(inverse, 2, c)
@@ -691,14 +818,38 @@
 
     @pl.loop(0, 3)
     def _(c):
-        leave(field, smoothed_out, c)
-
-    slot = (steps + 1) % 2
+        leave(field, guess_in, c)
+        loads.put(0, smoothed_out, c).start()
 
     @pl.loop(0, 3)
     def _(c):
-        collect(resid, slot, c)
-        leave(resid, residual_out, c)
+        leave(resid, source_in, c)
+
+    edge_lines[...] = jnp.zeros(edge_lines.shape, jnp.float32)
+    slot = (steps + 1) % 2
+    wait_for(slot, every)
+    arrive_y(slot)
+    arrive_x(slot)
+    for c in range(3):
+        for t in range(DEG):
+            edge_lines[c, 0, pl.ds(t, elems_y, stride=DEG), :] = arrived_x[c, t, 0:elems_y, :]
+            edge_lines[c, 1, pl.ds(t, elems_x, stride=DEG), :] = arrived_y[c, t, 0:elems_x, :]
+        edge_lines[c, 1, 0:1, :] = jnp.zeros((1, 128), jnp.float32)
+    depth = edge_lines.shape[2]
+    parts = halves(edge_lines[...].reshape(6 * depth, 128))
+    found = jnp.dot(
+        jnp.concatenate(parts, axis=1), select_in[...], preferred_element_type=jnp.float32
+    ).reshape(3, 2, depth, 128)
+    for c in range(3):
+        pieces = [found[c, 0, y : y + 1, 0:nodes_z] for y in range(nodes_y)]
+        source_in[c, 0:1, :] = source_in[c, 0:1, :] + jnp.concatenate(pieces, axis=1)
+        source_in[c, :, 0:nodes_z] = source_in[c, :, 0:nodes_z] + found[c, 1, 0:nodes_x, 0:nodes_z]
+        loads.put(1, residual_out, c).start()
+
+    @pl.loop(0, 3)
+    def _(c):
+        loads.put(0, smoothed_out, c).wait()
+        loads.put(1, residual_out, c).wait()
 
 
 def z_join(blocks, clamped):
@@ -731,7 +882,7 @@
     exact_join = [[joined, np.zeros_like(joined)]] * 2
     own_mat = jnp.asarray(np.block(exact_pair(np.kron(eye_z, own_np_1.T))))
     back_np = np.kron(eye_z, derivative_np) @ join_np
-    back_mat = jnp.asarray(np.block(exact_join + exact_pair(back_np)))
+    back_mat = jnp.asarray(np.block(exact_join + exact_pair(-back_np)))
     scaled_np = np.kron(eye_z, second_np) @ join_np
     second_mat = jnp.asarray(np.block(exact_join + exact_pair(scaled_np)))
     exact_mat = jnp.asarray(np.concatenate([joined, joined], axis=0))
@@ -768,40 +919,20 @@
 
     pad_x = -(-DEG * elems_x // 8) * 8
     whole = (3, N1, N1, cols, lanes)
-    vmem = pl.BlockSpec(memory_space=pltpu.VMEM)
     smem = pl.BlockSpec(memory_space=pltpu.SMEM)
     big = pltpu.VMEM(whole, jnp.float32)
     small = pltpu.VMEM((N1, N1, cols, lanes), jnp.float32)
-    face = pltpu.VMEM((2, 3, N1, cols, lanes), jnp.float32)
+    ring = 2 * elems_x
+    face_a = pltpu.VMEM((3, N1, 2 * elems_y, lanes), jnp.float32)
+    face_b = pltpu.VMEM((3, N1, ring, lanes), jnp.float32)
+    edge_size = -(-DEG * max(elems_x, elems_y) // 8) * 8
     lines = pltpu.VMEM((DEG * elems_y, pad_x, lanes), jnp.float32)
-    face_x = pltpu.VMEM((SLOTS, 3, 2, N1, elems_y, lanes), jnp.float32)
-    face_y = pltpu.VMEM((SLOTS, 3, 2, N1, elems_x, lanes), jnp.float32)
-    corner = pltpu.VMEM((SLOTS, 3, 4, 1, lanes), jnp.float32)
+    face_x = pltpu.VMEM((SLOTS, 2, 3, N1, elems_y, lanes), jnp.float32)
+    face_y = pltpu.VMEM((SLOTS, 2, 3, N1, elems_x, lanes), jnp.float32)
+    corner = pltpu.VMEM((SLOTS, 4, 3, 1, lanes), jnp.float32)
     shape = jax.ShapeDtypeStruct(guess.shape, jnp.float32)
 
-    def kernel(*refs):
-        smoother_kernel(SWEEPS * CHEB, elems_x, elems_y, *refs)
-
-    return pl.pallas_call(
-        kernel,
-        out_shape=(shape, shape),
-        in_specs=[smem] * 3 + [vmem] * 15,
-        out_specs=(vmem, vmem),
-        scratch_shapes=[pltpu.VMEM((3, SWEEPS * CHEB + 1, 1, lanes), jnp.float32)]
-        + [big] * 3
-        + [small] * 2
-        + [big] * 3
-        + [small] * 3
-        + [face] * 2
-        + [pltpu.VMEM((2, 4, N1, cols, lanes), jnp.float32)]
-        + [lines] * 2
-        + [face_x, face_y, corner] * 2
-        + [pltpu.SemaphoreType.DMA((SLOTS, 3, 8))] * 2,
-        compiler_params=pltpu.CompilerParams(collective_id=0, has_side_effects=True),
-    )(
-        lame,
-        upper,
-        lower_ratio,
+    operands = [
         guess,
         right_side,
         material,
@@ -817,7 +948,41 @@
         second_mat,
         exact_mat,
         join_in,
-    )
+    ]
+    number = len(operands)
+
+    def kernel(*refs):
+        scalars, places, outs = refs[:3], refs[3 : 3 + number], refs[3 + number : 5 + number]
+        staged, rest = refs[5 + number : 5 + 2 * number], refs[5 + 2 * number :]
+        loads = Loads(places, staged, *rest[:3])
+        smoother_kernel(SWEEPS * CHEB, elems_x, elems_y, *scalars, loads, *outs, *rest[3:])
+
+    away = pl.BlockSpec(memory_space=pl.ANY)
+    return pl.pallas_call(
+        kernel,
+        out_shape=(shape, shape),
+        in_specs=[smem] * 3 + [away] * number,
+        out_specs=(away, away),
+        scratch_shapes=[pltpu.VMEM(operand.shape, operand.dtype) for operand in operands]
+        + [pltpu.SemaphoreType.DMA((2, 3)), pltpu.SemaphoreType.DMA((number,)), pltpu.SemaphoreType.DMA((2, 3))]
+        + [pltpu.VMEM((3, SWEEPS * CHEB + 1, 1, lanes), jnp.float32)]
+        + [big] * 3
+        + [small] * 2
+        + [big] * 3
+        + [small] * 3
+        + [face_a, face_b] * 2
+        + [pltpu.VMEM((4, N1, cols, lanes), jnp.float32)]
+        + [pltpu.VMEM((2, 4, N1, ring, lanes), jnp.float32)]
+        + [face_a] * 2
+        + [pltpu.VMEM((6, N1, 2 * elems_y, lanes), jnp.float32)]
+        + [pltpu.VMEM((6, N1, cols, lanes), jnp.float32)]
+        + [pltpu.VMEM((2, 2, N1, ring, lanes), jnp.float32)]
+        + [pltpu.VMEM((3, 2, edge_size, lanes), jnp.float32)]
+        + [lines] * 2
+        + [face_x, face_y, corner] * 2
+        + [pltpu.SemaphoreType.DMA((SLOTS, 8))] * 2,
+        compiler_params=pltpu.CompilerParams(collective_id=0, has_side_effects=True),
+    )(lame, upper, lower_ratio, *operands)
 
 
 def solution(mesh):

time: 66.8 us -> 59.7 us (0.89)
  Pallas kernels: 61 us -> 54 us
    pallas_call x1, Pallas kernels: 61 us -> 54 us  [local(): pl.pallas_call(kernel, out_shape=(shape, shape), in_specs=[smem] * 3 + [a...]
where the time goes in v3:
time: 59.7 us; the launch traced here: 59.5 us
  Pallas kernels  54 us (90%)
  local copies, waits for them, and re-layouts  3.53 us (6%)
  between operations  1.94 us (3%)
    pallas_call x1, Pallas kernels, local(): pl.pallas_call(kernel, out_shape=(shape, shape), in_specs=[smem] * 3 + [a...  54 us
    unnamed x4, local copies, waits for them, and re-layouts  3.53 us

profile of v3, /device:TPU:0, one launch (start us, length us, event | category | flops | bytes accessed | tf_op | source)
XLA Modules:
  0.0 59.5 jit_solution(16463018957993091618)
XLA Ops:
  1.9 54.0 %shard_map.185 = (f32[3,28,3108]{2,1,0:T(8,128)}, f32[3,28,3108]{2,1,0:T(8,128)}) custom-call(f32[2,8]{1,0:T(2,128)} %refs_0_.1, f32[1]{0:T(128)S(6)} %copy.22.refs_1_, f32[1]{0:T(128)S(6)} %copy.23.refs_2_, f32[3,28,3108]{2,1,0:T(8,128)} %refs_3_.1, f32[3,28,3108]{2,1,0:T(8,128)} %refs_4_.1, s32[4,4,16]{2,1,0:T(4,128)} %refs_5_.1, ...), custom_call_target="tpu_custom_call" | custom-call | tf_op jit(solution)/shard_map/pallas_call | solution.py:961
  56.0 0.0 copy-start
  56.0 2.5 %copy.24 = f32[3,28,3108]{2,1,0:T(8,128)} copy(f32[3,28,3108]{2,1,0:T(8,128)} %get-tuple-element.4) | data formatting | bytes 2088576
  58.5 0.0 copy-done
  58.5 1.0 %copy.25 = f32[3,28,3108]{2,1,0:T(8,128)} copy(f32[3,28,3108]{2,1,0:T(8,128)S(1)} %copy-done) | data formatting | bytes 2088576
Async XLA Ops:
  56.0 2.5 %copy-start = (f32[3,28,3108]{2,1,0:T(8,128)S(1)}, f32[3,28,3108]{2,1,0:T(8,128)}, u32[]{:S(2)}) copy-start(f32[3,28,3108]{2,1,0:T(8,128)} %get-tuple-element.5) | copy-start | bytes 3132868

commit v4 on v3

--- a/solution.py
+++ b/solution.py
@@ -55,6 +55,7 @@
 N1 = DEG + 1
 SLOTS = 3
 UNROLL = 6
+VMEM_BYTES = 36 * 1024 * 1024
 
 
 def halves(value):
@@ -95,12 +96,11 @@
 
 
 class Loads:
-    def __init__(self, places, staged, part_sem, whole_sem, put_sem):
+    def __init__(self, places, staged, part_sem, whole_sem):
         self.places = places
         self.staged = staged
         self.part_sem = part_sem
         self.whole_sem = whole_sem
-        self.put_sem = put_sem
 
     def part(self, at, c):
         return pltpu.make_async_copy(
@@ -109,9 +109,6 @@
 
     def whole(self, at):
         return pltpu.make_async_copy(self.places[at], self.staged[at], self.whole_sem.at[at])
-
-    def put(self, at, out, c):
-        return pltpu.make_async_copy(self.staged[at].at[c], out.at[c], self.put_sem.at[at, c])
 
     def start(self):
         self.whole(7).start()
@@ -140,6 +137,7 @@
     loads,
     smoothed_out,
     residual_out,
+    patch_out,
     coef,
     field,
     resid,
@@ -818,12 +816,11 @@
 
     @pl.loop(0, 3)
     def _(c):
-        leave(field, guess_in, c)
-        loads.put(0, smoothed_out, c).start()
+        leave(field, smoothed_out, c)
 
     @pl.loop(0, 3)
     def _(c):
-        leave(resid, source_in, c)
+        leave(resid, residual_out, c)
 
     edge_lines[...] = jnp.zeros(edge_lines.shape, jnp.float32)
     slot = (steps + 1) % 2
@@ -839,17 +836,25 @@
     parts = halves(edge_lines[...].reshape(6 * depth, 128))
     found = jnp.dot(
         jnp.concatenate(parts, axis=1), select_in[...], preferred_element_type=jnp.float32
-    ).reshape(3, 2, depth, 128)
+    )
+    patch_out[...] = found.reshape(patch_out.shape)
+
+
+def finish(nodes_z, nodes_x, nodes_y, smoothed_in, residual_in, patch_in, smoothed_out, residual_out, held, put_sem):
+    def put(at, source, target, c):
+        return pltpu.make_async_copy(source.at[c], target.at[c], put_sem.at[at, c])
+
     for c in range(3):
-        pieces = [found[c, 0, y : y + 1, 0:nodes_z] for y in range(nodes_y)]
-        source_in[c, 0:1, :] = source_in[c, 0:1, :] + jnp.concatenate(pieces, axis=1)
-        source_in[c, :, 0:nodes_z] = source_in[c, :, 0:nodes_z] + found[c, 1, 0:nodes_x, 0:nodes_z]
-        loads.put(1, residual_out, c).start()
-
-    @pl.loop(0, 3)
-    def _(c):
-        loads.put(0, smoothed_out, c).wait()
-        loads.put(1, residual_out, c).wait()
+        put(0, smoothed_in, smoothed_out, c).start()
+    for c in range(3):
+        pieces = [patch_in[c, 0, y : y + 1, 0:nodes_z] for y in range(nodes_y)]
+        held[c] = residual_in[c]
+        held[c, 0:1, :] = held[c, 0:1, :] + jnp.concatenate(pieces, axis=1)
+        held[c, :, 0:nodes_z] = held[c, :, 0:nodes_z] + patch_in[c, 1, 0:nodes_x, 0:nodes_z]
+        put(1, held, residual_out, c).start()
+    for c in range(3):
+        put(0, smoothed_in, smoothed_out, c).wait()
+        put(1, held, residual_out, c).wait()
 
 
 def z_join(blocks, clamped):
@@ -952,19 +957,22 @@
     number = len(operands)
 
     def kernel(*refs):
-        scalars, places, outs = refs[:3], refs[3 : 3 + number], refs[3 + number : 5 + number]
-        staged, rest = refs[5 + number : 5 + 2 * number], refs[5 + 2 * number :]
-        loads = Loads(places, staged, *rest[:3])
-        smoother_kernel(SWEEPS * CHEB, elems_x, elems_y, *scalars, loads, *outs, *rest[3:])
+        scalars, places, outs = refs[:3], refs[3 : 3 + number], refs[3 + number : 6 + number]
+        staged, rest = refs[6 + number : 6 + 2 * number], refs[6 + 2 * number :]
+        loads = Loads(places, staged, *rest[:2])
+        smoother_kernel(SWEEPS * CHEB, elems_x, elems_y, *scalars, loads, *outs, *rest[2:])
 
     away = pl.BlockSpec(memory_space=pl.ANY)
-    return pl.pallas_call(
+    vmem = pl.BlockSpec(memory_space=pltpu.VMEM)
+    operands = [pltpu.with_memory_space_constraint(operand, pltpu.HBM) for operand in operands]
+    patch_shape = (3, 2, edge_size, lanes)
+    results = pl.pallas_call(
         kernel,
-        out_shape=(shape, shape),
+        out_shape=(shape, shape, jax.ShapeDtypeStruct(patch_shape, jnp.float32)),
         in_specs=[smem] * 3 + [away] * number,
-        out_specs=(away, away),
+        out_specs=(vmem, vmem, vmem),
         scratch_shapes=[pltpu.VMEM(operand.shape, operand.dtype) for operand in operands]
-        + [pltpu.SemaphoreType.DMA((2, 3)), pltpu.SemaphoreType.DMA((number,)), pltpu.SemaphoreType.DMA((2, 3))]
+        + [pltpu.SemaphoreType.DMA((2, 3)), pltpu.SemaphoreType.DMA((number,))]
         + [pltpu.VMEM((3, SWEEPS * CHEB + 1, 1, lanes), jnp.float32)]
         + [big] * 3
         + [small] * 2
@@ -977,12 +985,26 @@
         + [pltpu.VMEM((6, N1, 2 * elems_y, lanes), jnp.float32)]
         + [pltpu.VMEM((6, N1, cols, lanes), jnp.float32)]
         + [pltpu.VMEM((2, 2, N1, ring, lanes), jnp.float32)]
-        + [pltpu.VMEM((3, 2, edge_size, lanes), jnp.float32)]
+        + [pltpu.VMEM(patch_shape, jnp.float32)]
         + [lines] * 2
         + [face_x, face_y, corner] * 2
         + [pltpu.SemaphoreType.DMA((SLOTS, 8))] * 2,
-        compiler_params=pltpu.CompilerParams(collective_id=0, has_side_effects=True),
-    )(lame, upper, lower_ratio, *operands)
+        compiler_params=pltpu.CompilerParams(
+            collective_id=0, has_side_effects=True, vmem_limit_bytes=VMEM_BYTES
+        ),
+    )(pltpu.with_memory_space_constraint(lame, pltpu.HBM), upper, lower_ratio, *operands)
+
+    def finish_kernel(*refs):
+        finish(nodes_z, DEG * elems_x, DEG * elems_y, *refs)
+
+    return pl.pallas_call(
+        finish_kernel,
+        out_shape=(shape, shape),
+        in_specs=[vmem] * 3,
+        out_specs=(away, away),
+        scratch_shapes=[pltpu.VMEM(guess.shape, jnp.float32), pltpu.SemaphoreType.DMA((2, 3))],
+        compiler_params=pltpu.CompilerParams(vmem_limit_bytes=VMEM_BYTES // 2),
+    )(*results)
 
 
 def solution(mesh):

time: 59.7 us -> 56.5 us (0.946)
  local copies, waits for them, and re-layouts: 3.53 us -> 0 us
    unnamed x4 -> x0, local copies, waits for them, and re-layouts: 3.53 us -> none
    pallas_call x1 -> x2, Pallas kernels: 54 us -> 54.4 us  [the longest x1 52.9 us: local(): pl.pallas_call(kernel, out_shape=(shape, shape, jax.ShapeDtypeStruct(patc...]
where the time goes in v4:
time: 56.5 us; the launch traced here: 56.3 us
  Pallas kernels  54.4 us (96%)
  between operations  1.93 us (3%)
    pallas_call x1, Pallas kernels, local(): pl.pallas_call(kernel, out_shape=(shape, shape, jax.ShapeDtypeStruct(patc...  52.9 us
    pallas_call x1, Pallas kernels, local(): pl.pallas_call(finish_kernel, out_shape=(shape, shape), in_specs=[vmem] *...  1.5 us

profile of v4, /device:TPU:0, one launch (start us, length us, event | category | flops | bytes accessed | tf_op | source)
XLA Modules:
  0.0 56.3 jit_solution(6068098193838196023)
XLA Ops:
  1.9 52.9 %shard_map.185 = (f32[3,28,3108]{2,1,0:T(8,128)S(1)}, f32[3,28,3108]{2,1,0:T(8,128)S(1)}, f32[3,2,32,128]{3,2,1,0:T(8,128)S(1)}) custom-call(f32[2,8]{1,0:T(2,128)} %refs_0_.1, f32[1]{0:T(128)S(6)} %copy.20.refs_1_, f32[1]{0:T(128)S(6)} %copy.21.refs_2_, f32[3,28,3108]{2,1,0:T(8,128)} %refs_3_.1, f32[3,28,3108]{2,1,0:T(8,128)} %refs_4_.1, ...), custom_call_target="tpu_custom_call" | custom-call | tf_op jit(solution)/shard_map/pallas_call | solution.py:969
  54.8 1.5 %shard_map.186 = (f32[3,28,3108]{2,1,0:T(8,128)}, f32[3,28,3108]{2,1,0:T(8,128)}) custom-call(f32[3,28,3108]{2,1,0:T(8,128)S(1)} %get-tuple-element.5.refs_0_, f32[3,28,3108]{2,1,0:T(8,128)S(1)} %get-tuple-element.6.refs_1_, f32[3,2,32,128]{3,2,1,0:T(8,128)S(1)} %get-tuple-element.7.refs_2_), custom_call_target="tpu_custom_call" | custom-call | tf_op jit(solution)/shard_map/pallas_call | solution.py:1000

commit v5 on v4

--- a/solution.py
+++ b/solution.py
@@ -757,6 +757,13 @@
                             change_by = rank_y[w, kind, p] * first[t] + rank_y[w, kind + 1, p] * then[t]
                             resid[c, t, p, rows] = resid[c, t, p, rows] - change_by
 
+    for c in range(3):
+        fill(field, 0, c)
+
+    pl.semaphore_wait(barrier, len(partners))
+
+    start_all(0, every)
+
     @pl.loop(0, 3)
     def _(c):
         loads.wait_part(1, c)
@@ -775,12 +782,8 @@
             resid[c, i] = zeros_big
 
     for c in range(3):
-        fill(field, 0, c)
         fill(inverse, 2, c)
 
-    pl.semaphore_wait(barrier, len(partners))
-
-    start_all(0, every)
     start_all(2, every)
 
     @pl.loop(0, steps + 1)

time: 56.5 us -> 55 us (0.973)
  Pallas kernels: 54.4 us -> 52.9 us
    pallas_call x1, Pallas kernels: 52.9 us -> 51.4 us  [local(): pl.pallas_call(kernel, out_shape=(shape, shape, jax.ShapeDtypeStruct(patc...]
where the time goes in v5:
time: 55 us; the launch traced here: 54.8 us
  Pallas kernels  52.9 us (96%)
  between operations  1.93 us (4%)
    pallas_call x1, Pallas kernels, local(): pl.pallas_call(kernel, out_shape=(shape, shape, jax.ShapeDtypeStruct(patc...  51.4 us
    pallas_call x1, Pallas kernels, local(): pl.pallas_call(finish_kernel, out_shape=(shape, shape), in_specs=[vmem] *...  1.5 us

profile of v5, /device:TPU:0, one launch (start us, length us, event | category | flops | bytes accessed | tf_op | source)
XLA Modules:
  0.0 54.8 jit_solution(7799568199927461565)
XLA Ops:
  1.9 51.4 %shard_map.185 = (f32[3,28,3108]{2,1,0:T(8,128)S(1)}, f32[3,28,3108]{2,1,0:T(8,128)S(1)}, f32[3,2,32,128]{3,2,1,0:T(8,128)S(1)}) custom-call(f32[2,8]{1,0:T(2,128)} %refs_0_.1, f32[1]{0:T(128)S(6)} %copy.20.refs_1_, f32[1]{0:T(128)S(6)} %copy.21.refs_2_, f32[3,28,3108]{2,1,0:T(8,128)} %refs_3_.1, f32[3,28,3108]{2,1,0:T(8,128)} %refs_4_.1, ...), custom_call_target="tpu_custom_call" | custom-call | tf_op jit(solution)/shard_map/pallas_call | solution.py:972
  53.3 1.5 %shard_map.186 = (f32[3,28,3108]{2,1,0:T(8,128)}, f32[3,28,3108]{2,1,0:T(8,128)}) custom-call(f32[3,28,3108]{2,1,0:T(8,128)S(1)} %get-tuple-element.5.refs_0_, f32[3,28,3108]{2,1,0:T(8,128)S(1)} %get-tuple-element.6.refs_1_, f32[3,2,32,128]{3,2,1,0:T(8,128)S(1)} %get-tuple-element.7.refs_2_), custom_call_target="tpu_custom_call" | custom-call | tf_op jit(solution)/shard_map/pallas_call | solution.py:1003
